TPU v7x, 16 devices: a whole 2x2x2 slice. The times are simulated.
16 devices in a mesh: col: 4 (over z, y), row: 4 (over x, core).
Axes of the slice: x: 2, y: 2, z: 2, core: 2. Of those that a mesh axis runs over, the one named last changes fastest.
Arguments:
- image: bfloat16 [1, 512, 512, 128], P(None, 'row', 'col')
- w_first: bfloat16 [3, 3, 128, 128], replicated
- w_second: bfloat16 [3, 3, 128, 128], replicated
- w_third: bfloat16 [3, 3, 128, 128], replicated
- grad_out: bfloat16 [1, 512, 512, 128], P(None, 'row', 'col')
Outputs:
- output 1: bfloat16 [1, 512, 512, 128], P(None, 'row', 'col')
- output 2: bfloat16 [1, 512, 512, 128], P(None, 'row', 'col')
- output 3: float32 [3, 3, 128, 128], replicated
- output 4: float32 [3, 3, 128, 128], replicated
- output 5: float32 [3, 3, 128, 128], replicated
All inputs are finite; a program needn't handle non-finite values.
Results may differ from a plain program's by a relative error of at most 0.0141409.
Values are sent between devices in bfloat16 or wider.
A program may use at most 1 GiB of HBM per device.

v0:
```python
import math
import jax
import jax.numpy as jnp
from jax import lax
from jax.sharding import PartitionSpec as P

GELU_SCALE = math.sqrt(2.0 / math.pi)
GELU_CUBIC = 0.044715
CONV_DIMS = ('NHWC', 'HWIO', 'NHWC')
BACK_DIMS = ('NHWC', 'HWOI', 'NHWC')
WGRAD_DIMS = ('CHWN', 'IHWO', 'HWNC')


def gelu_tanh(value):
    return 0.5 * value * (1.0 + jnp.tanh(GELU_SCALE * (value + GELU_CUBIC * value * value * value)))


def gelu_slope(value):
    tanh_val = jnp.tanh(GELU_SCALE * (value + GELU_CUBIC * value * value * value))
    return 0.5 * (1.0 + tanh_val) + 0.5 * value * (1.0 - tanh_val * tanh_val) * GELU_SCALE * (1.0 + 3.0 * GELU_CUBIC * value * value)


def conv_valid(padded, weight):
    return lax.conv_general_dilated(padded, weight, (1, 1), 'VALID', dimension_numbers=CONV_DIMS, preferred_element_type=jnp.float32)


def conv_back(padded_grad, weight):
    return lax.conv_general_dilated(padded_grad, lax.rev(weight, (0, 1)), (1, 1), 'VALID', dimension_numbers=BACK_DIMS, preferred_element_type=jnp.float32)


def weight_grad(padded, grad):
    return lax.conv_general_dilated(padded, grad, (1, 1), 'VALID', dimension_numbers=WGRAD_DIMS, preferred_element_type=jnp.float32)


def border_pad(tile, width, n_rows, n_cols):
    down_pairs = [(source, source + 1) for source in range(n_rows - 1)]
    up_pairs = [(source + 1, source) for source in range(n_rows - 1)]
    from_above = lax.ppermute(tile[:, tile.shape[1] - width:], 'row', down_pairs)
    from_below = lax.ppermute(tile[:, :width], 'row', up_pairs)
    taller = jnp.concatenate([from_above, tile, from_below], axis=1)
    right_pairs = [(source, source + 1) for source in range(n_cols - 1)]
    left_pairs = [(source + 1, source) for source in range(n_cols - 1)]
    from_left = lax.ppermute(taller[:, :, taller.shape[2] - width:], 'col', right_pairs)
    from_right = lax.ppermute(taller[:, :, :width], 'col', left_pairs)
    return jnp.concatenate([from_left, taller, from_right], axis=2)


def solution(mesh):
    n_rows = mesh.shape['row']
    n_cols = mesh.shape['col']
    act_spec = P(None, 'row', 'col', None)

    def pad_one(tile):
        return border_pad(tile, 1, n_rows, n_cols)

    def forward_acts(image, w_first, w_second):
        img_pad = pad_one(image)
        pre_one = conv_valid(img_pad, w_first).astype(jnp.bfloat16)
        one_pad = pad_one(gelu_tanh(pre_one.astype(jnp.float32)).astype(jnp.bfloat16))
        pre_two = conv_valid(one_pad, w_second).astype(jnp.bfloat16)
        two_pad = pad_one(gelu_tanh(pre_two.astype(jnp.float32)).astype(jnp.bfloat16))
        return img_pad, pre_one, one_pad, pre_two, two_pad

    def local_block(image, w_first, w_second, w_third, grad_out):
        fwd_two_pad = forward_acts(image, w_first, w_second)[4]
        block_out = (conv_valid(fwd_two_pad, w_third) + image.astype(jnp.float32)).astype(jnp.bfloat16)
        img_pad, pre_one, one_pad, pre_two, two_pad = forward_acts(image, w_first, w_second)
        grad_pad = pad_one(grad_out)
        grad_pre2 = (conv_back(grad_pad, w_third) * gelu_slope(pre_two.astype(jnp.float32))).astype(jnp.bfloat16)
        grad_w_third = lax.psum(weight_grad(two_pad, grad_out), ('row', 'col'))
        pre2_pad = pad_one(grad_pre2)
        grad_pre1 = (conv_back(pre2_pad, w_second) * gelu_slope(pre_one.astype(jnp.float32))).astype(jnp.bfloat16)
        grad_w_second = lax.psum(weight_grad(one_pad, grad_pre2), ('row', 'col'))
        pre1_pad = pad_one(grad_pre1)
        grad_image = (conv_back(pre1_pad, w_first) + grad_out.astype(jnp.float32)).astype(jnp.bfloat16)
        grad_w_first = lax.psum(weight_grad(img_pad, grad_pre1), ('row', 'col'))
        return block_out, grad_image, grad_w_first, grad_w_second, grad_w_third

    return jax.shard_map(local_block, mesh=mesh, in_specs=(act_spec, P(), P(), P(), act_spec), out_specs=(act_spec, act_spec, P(), P(), P()), check_vma=False)
```

profile of v0, /device:TPU:0, one launch (start us, length us, event | category | flops | bytes accessed | tf_op | source)
XLA Modules:
  0.0 523.6 jit_solution(1372349461018947987)
XLA Ops:
  8.2 2.8 collective-permute-start
  10.9 1.3 collective-permute-start.1
  13.0 5.1 collective-permute-start.12
  18.2 1.3 collective-permute-start.13
  19.5 3.0 constant_dynamic-update-slice_fusion.1
  22.7 3.4 collective-permute-start.2
  26.1 1.3 collective-permute-start.3
  28.2 4.5 collective-permute-start.14
  32.7 1.3 collective-permute-start.15
  34.1 2.2 maximum_bitcast_fusion
  37.7 2.2 copy-done.2
  40.9 14.1 %fusion.32 = (bf16[128,8,17,128]{3,1,2,0:T(8,128)(2,1)S(1)}, bf16[128,8,17,128]{3,1,2,0:T(8,128)(2,1)}) fusion(bf16[3,3,128,128]{3,2,1,0:T(8,128)(2,1)S(1)} %copy-done.23, bf16[130,1,7,2,128]{4,2,3,0,1:T(8,128)(2,1)S(1)} %slice.150, bf16[130,1,8,17,128]{4,2,3,0,1:T(8,128)(2,1)S(1)} %copy.17, pred[8,17]{0,1:T(8,128)(4,1)S(1)} %copy-done.25), kind=kOutput, calls=%fused_computation.48 | convolution fusion | flops 5175742464 | bytes 14199944 | tf_op jit(solution)/shard_map/conv_general_dilated | solution.py:24
  54.9 3.3 copy.19
  58.5 1.3 collective-permute-start.5
  59.9 4.7 collective-permute-start.4
  64.5 2.5 slice_bitcast_fusion.5
  67.0 2.8 fusion.157
  71.0 3.1 fusion.94
  74.2 5.0 collective-permute-start.6
  79.2 1.3 collective-permute-start.7
  80.6 2.2 maximum_bitcast_fusion.2
  85.9 2.8 copy.60
  88.7 3.9 maximum_bitcast_fusion.1
  96.2 14.0 %fusion.26 = (bf16[128,8,17,128]{3,1,2,0:T(8,128)(2,1)S(1)}, bf16[128,8,17,128]{3,1,2,0:T(8,128)(2,1)}) fusion(bf16[3,3,128,128]{3,2,1,0:T(8,128)(2,1)S(1)} %copy-done, bf16[130,1,7,2,128]{4,2,3,0,1:T(8,128)(2,1)S(1)} %slice.156, bf16[130,1,8,17,128]{4,2,3,0,1:T(8,128)(2,1)S(1)} %copy.24, pred[8,17]{0,1:T(8,128)(4,1)S(1)} %copy-done.25), kind=kOutput, calls=%fused_computation.42 | convolution fusion | flops 5175742464 | bytes 14199944 | tf_op jit(solution)/shard_map/conv_general_dilated | solution.py:24
  110.3 17.1 %fusion.31 = bf16[128,8,17,128]{3,1,2,0:T(8,128)(2,1)S(1)} fusion(bf16[128,8,17,128]{3,1,2,0:T(8,128)(2,1)} %get-tuple-element.48, pred[8,17]{0,1:T(8,128)(4,1)S(1)} %copy-done.25, bf16[3,3,128,128]{3,2,1,0:T(8,128)(2,1)S(1)} %copy-done.21, bf16[130,1,7,2,128]{4,2,3,0,1:T(8,128)(2,1)S(1)} %slice.168, bf16[130,1,8,17,128]{4,2,3,0,1:T(8,128)(2,1)S(1)} %copy.39), kind=kOutput, calls=%fused_computation.47 | convolution fusion | flops 5195796480 | bytes 14199944 | tf_op jit(solution)/shard_map/conv_general_dilated | solution.py:28
  129.2 3.3 copy.27
  132.5 2.7 fusion.156
  135.3 3.2 slice.188
  138.4 2.7 copy.66
  141.2 2.3 slice_bitcast_fusion.3
  146.2 5.4 %collective-permute-start.16 = (bf16[1,1,128,128]{3,2,1,0:T(8,128)(2,1)}, bf16[1,1,128,128]{3,2,1,0:T(8,128)(2,1)}, u32[]{:S(2)}, u32[]{:S(2)}) collective-permute-start(bf16[1,1,128,128]{3,2,1,0:T(8,128)(2,1)} %slice.170), channel_id=1, source_target_pairs={{0,1},{1,2},{2,3},{4,5},{5,6},{6,7},{8,9},{9,10},{10,11},{12,13},{... | collective-permute-start | bytes 98312 | tf_op jit(solution)/shard_map/ppermute | solution.py:38
  152.3 4.0 collective-permute-start.8
  156.4 5.2 fusion.97
  161.6 23.1 %fusion.124 = f32[3,3,128,128]{3,2,1,0:T(8,128)} fusion(bf16[128,8,17,128]{3,1,2,0:T(8,128)(2,1)} %copy-done.14, pred[8,17]{0,1:T(8,128)(4,1)S(1)} %copy-done.25, bf16[130,8,17,128,1]{3,1,4,2,0:T(8,128)(2,1)} %fusion.97, bf16[130,8,17,128,1]{3,1,4,2,0:T(8,128)(2,1)} %get-tuple-element.15, bf16[130,8,17,128,1]{3,1,4,2,0:T(8,128)(2,1)} %copy.66), kind=kOutput, calls=%fused_computation.140 | convolution fusion | flops 5149634560 | bytes 18624648 | tf_op jit(solution)/shard_map/conv_general_dilated | solution.py:32
  184.7 4.8 slice_bitcast_fusion.4
  189.6 1.6 collective-permute-start.9
  192.9 5.5 %collective-permute-start.18 = (bf16[1,130,1,128]{3,1,2,0:T(8,128)(2,1)S(1)}, bf16[1,130,1,128]{3,1,2,0:T(8,128)(2,1)S(1)}, u32[]{:S(2)}, u32[]{:S(2)}) collective-permute-start(bf16[1,130,1,128]{3,1,2,0:T(8,128)(2,1)S(1)} %get-tuple-element.33), channel_id=1, source_target_pairs={{0,4},{4,8},{8,12},{1,5},{5,9},{9,13},{2,6},{6,10},{10,14},{3,7},{... | collective-permute-start | bytes 99848 | tf_op jit(solution)/shard_map/ppermute | solution.py:43
  200.6 18.1 %copy_dynamic-update-slice_fusion = bf16[1,130,128,128]{3,0,2,1:T(2,128)(2,1)S(1)} fusion(bf16[1,130,128,128]{3,0,2,1:T(2,128)(2,1)S(1)} %constant_dynamic-update-slice_fusion.4, bf16[1,128,128,128]{3,1,2,0:T(8,128)(2,1)S(1)} %copy-done.11), kind=kLoop, calls=%fused_computation.69 | loop fusion | bytes 12582912
  219.0 5.2 collective-permute-start.10
  225.5 4.8 maximum_bitcast_fusion.3
  232.7 15.7 %fusion.37 = bf16[128,8,17,128]{3,1,2,0:T(8,128)(2,1)S(1)} fusion(bf16[128,8,17,128]{3,1,2,0:T(8,128)(2,1)S(1)} %bitcast.138, pred[8,17]{0,1:T(8,128)(4,1)S(1)} %copy-done.25, bf16[3,3,128,128]{3,2,1,0:T(8,128)(2,1)S(1)} %copy-done, bf16[130,1,7,2,128]{4,2,3,0,1:T(8,128)(2,1)S(1)} %slice.174, bf16[130,1,8,17,128]{4,2,3,0,1:T(8,128)(2,1)S(1)} %copy.46), kind=kOutput, calls=%fused_computation.53 | convolution fusion | flops 5195796480 | bytes 14199944 | tf_op jit(solution)/shard_map/conv_general_dilated | solution.py:28
  249.1 3.2 copy.48
  252.4 24.4 %pad_maximum_fusion = bf16[1,130,130,128]{3,0,2,1:T(2,128)(2,1)S(1)} fusion(bf16[1,130,1,128]{3,0,2,1:T(2,128)(2,1)S(1)} %collective-permute-done.11, bf16[1,130,128,128]{3,0,2,1:T(2,128)(2,1)} %copy-done.12, bf16[1,130,1,128]{3,0,2,1:T(2,128)(2,1)S(1)} %collective-permute-done.10), kind=kLoop, calls=%fused_computation.62 | loop fusion | flops 4326400 | bytes 8652800 | tf_op jit(solution)/shard_map/concatenate | solution.py:45
  276.7 76.7 %fusion.48 = f32[3,3,128,128]{3,2,1,0:T(8,128)} fusion(bf16[1,130,130,128]{3,0,2,1:T(2,128)(2,1)S(1)} %pad_maximum_fusion, bf16[1,128,128,128]{3,2,1,0:T(8,128)(2,1)S(1)} %copy-done.9), kind=kOutput, calls=%fused_computation.70 | convolution fusion | flops 4831838208 | bytes 9110528 | tf_op jit(solution)/shard_map/conv_general_dilated | solution.py:32
  353.4 2.8 copy.84
  358.9 3.9 collective-permute-start.20
  362.7 2.9 copy.76
  367.4 13.2 %broadcast_select_fusion.1 = f32[128,8,17,128]{3,1,2,0:T(8,128)} fusion(pred[8,17]{0,1:T(8,128)(4,1)S(1)} %copy-done.26, bf16[3,3,128,128]{3,2,1,0:T(8,128)(2,1)S(1)} %copy-done.22, bf16[130,1,7,2,128]{4,2,3,0,1:T(8,128)(2,1)S(1)} %slice.164, bf16[130,1,8,17,128]{4,2,3,0,1:T(8,128)(2,1)S(1)} %copy.34), kind=kOutput, calls=%fused_computation.125 | convolution fusion | flops 5151232000 | bytes 14199944 | tf_op jit(solution)/shard_map/conv_general_dilated | solution.py:24
  380.7 23.1 %fusion.129 = f32[3,3,128,128]{3,2,1,0:T(8,128)} fusion(bf16[128,8,17,128]{3,1,2,0:T(8,128)(2,1)} %copy-done.15, pred[8,17]{0,1:T(8,128)(4,1)S(1)} %copy-done.26, bf16[130,8,17,128,1]{3,1,4,2,0:T(8,128)(2,1)} %fusion.94, bf16[130,8,17,128,1]{3,1,4,2,0:T(8,128)(2,1)} %get-tuple-element.19, bf16[130,8,17,128,1]{3,1,4,2,0:T(8,128)(2,1)} %copy.60), kind=kOutput, calls=%fused_computation.141 | convolution fusion | flops 5149634560 | bytes 18624648 | tf_op jit(solution)/shard_map/conv_general_dilated | solution.py:32
  403.8 2.5 slice_bitcast_fusion.2
  406.3 6.8 %copy.35 = f32[128,8,17,128]{3,0,2,1:T(8,128)S(1)} copy(f32[128,8,17,128]{3,1,2,0:T(8,128)} %broadcast_select_fusion.1) | data formatting | bytes 17825792 | tf_op jit(solution)/shard_map/conv_general_dilated | solution.py:24
  415.0 5.4 %collective-permute-start.22 = (bf16[1,130,1,128]{3,1,2,0:T(8,128)(2,1)S(1)}, bf16[1,130,1,128]{3,1,2,0:T(8,128)(2,1)S(1)}, u32[]{:S(2)}, u32[]{:S(2)}) collective-permute-start(bf16[1,130,1,128]{3,1,2,0:T(8,128)(2,1)S(1)} %get-tuple-element.31), channel_id=1, source_target_pairs={{0,4},{4,8},{8,12},{1,5},{5,9},{9,13},{2,6},{6,10},{10,14},{3,7},{... | collective-permute-start | bytes 99848 | tf_op jit(solution)/shard_map/ppermute | solution.py:43
  420.4 1.3 collective-permute-start.23
  421.7 9.6 %fusion.47 = bf16[1,128,128,128]{3,1,2,0:T(8,128)(2,1)S(1)} fusion(f32[128,1,136,128]{3,0,2,1:T(8,128)S(1)} %bitcast.124, bf16[1,128,128,128]{3,2,1,0:T(8,128)(2,1)S(1)} %copy-done.7), kind=kLoop, calls=%fused_computation.68 | loop fusion | flops 6291456 | bytes 16777216 | tf_op jit(solution)/shard_map/convert_element_type | solution.py:66
  431.3 4.7 copy.70
  436.0 5.2 %maximum_bitcast_fusion.4 = bf16[130,1,130,128]{3,0,2,1:T(8,128)(2,1)S(1)} fusion(bf16[1,130,1,128]{3,1,2,0:T(8,128)(2,1)S(1)} %collective-permute-done.23, bf16[1,1,128,128]{3,1,2,0:T(2,128)(2,1)} %collective-permute-done.21, bf16[1,128,128,128]{3,1,2,0:T(8,128)(2,1)} %copy-done.4, bf16[1,1,128,128]{3,1,2,0:T(2,128)(2,1)S(1)} %copy.51, ...), kind=kLoop, calls=%fused_computation.118 | loop fusion | flops 21632000 | bytes 8652800 | tf_op jit(solution)/shard_map/concatenate | solution.py:45
  443.1 13.1 %broadcast_select_fusion = f32[128,8,17,128]{3,1,2,0:T(8,128)} fusion(pred[8,17]{0,1:T(8,128)(4,1)S(1)} %copy-done.26, bf16[3,3,128,128]{3,2,1,0:T(8,128)(2,1)S(1)} %copy-done.24, bf16[130,1,7,2,128]{4,2,3,0,1:T(8,128)(2,1)S(1)} %slice.180, bf16[130,1,8,17,128]{4,2,3,0,1:T(8,128)(2,1)S(1)} %copy.53), kind=kOutput, calls=%fused_computation.124 | convolution fusion | flops 5151232000 | bytes 14199944 | tf_op jit(solution)/shard_map/conv_general_dilated | solution.py:28
  456.2 5.4 %copy.54 = f32[128,8,17,128]{3,0,2,1:T(8,128)S(1)} copy(f32[128,8,17,128]{3,1,2,0:T(8,128)} %broadcast_select_fusion) | data formatting | bytes 17825792 | tf_op jit(solution)/shard_map/conv_general_dilated | solution.py:28
  461.6 9.8 %fusion.45 = bf16[1,128,128,128]{3,1,2,0:T(8,128)(2,1)S(1)} fusion(f32[128,1,136,128]{3,0,2,1:T(8,128)S(1)} %bitcast.125, bf16[1,128,128,128]{3,2,1,0:T(8,128)(2,1)S(1)} %copy-done.10), kind=kLoop, calls=%fused_computation.65 | loop fusion | flops 6291456 | bytes 16777216 | tf_op jit(solution)/shard_map/convert_element_type | solution.py:75
  471.5 4.7 copy.71
  476.2 34.3 %all-reduce.3.cloned.1.call-done = (f32[3,3,128,128]{3,2,1,0:T(8,128)}, f32[3,3,128,128]{3,2,1,0:T(8,128)}, f32[3,3,128,128]{3,2,1,0:T(8,128)}) async-done(((f32[3,3,128,128]{3,2,1,0:T(8,128)}, f32[3,3,128,128]{3,2,1,0:T(8,128)}, f32[3,3,128,128]{3,2,1,0:T(8,128)}), (f32[3,3,128,128]{3,2,1,0:T(8,128)}, f32[3,3,128,128]{3,2,1,0:T(8,128)}, f32[3,3,128,128]{3,2,1,0:T(8,128)})) %all-reduce.3.cloned.1.call-update) | async-done | bytes 1769488 | tf_op jit(solution)/shard_map/psum | solution.py:76
  510.5 1.9 copy.94
  512.4 1.9 copy.95
  514.4 1.9 copy.96
  (172 shorter events, 35.1 us)
Async XLA Ops:
  7.2 89.1 %copy-start = (bf16[3,3,128,128]{3,2,1,0:T(8,128)(2,1)S(1)}, bf16[3,3,128,128]{3,2,1,0:T(8,128)(2,1)}, u32[]{:S(2)}) copy-start(bf16[3,3,128,128]{3,2,1,0:T(8,128)(2,1)} %param.7) | copy-start | bytes 884740
  7.2 503.3 %all-reduce.3.cloned.1.call-start = ((), (), s32[]{:S(2)}) async-start(), calls=%async_computation | async-start | bytes 3538944 | tf_op jit(solution)/shard_map/psum | solution.py:76
  7.2 20.2 %copy-start.8 = (bf16[1,128,128,128]{3,2,1,0:T(8,128)(2,1)S(1)}, bf16[1,128,128,128]{3,2,1,0:T(8,128)(2,1)}, u32[]{:S(2)}) copy-start(bf16[1,128,128,128]{3,2,1,0:T(8,128)(2,1)} %param.9) | copy-start | bytes 12582916
  8.2 11.3 %collective-permute-start = (bf16[1,1,128,128]{3,2,1,0:T(8,128)(2,1)S(1)}, bf16[1,1,128,128]{3,2,1,0:T(8,128)(2,1)S(1)}, u32[]{:S(2)}, u32[]{:S(2)}) collective-permute-start(bf16[1,1,128,128]{3,2,1,0:T(8,128)(2,1)S(1)} %get-tuple-element.44), channel_id=1, source_target_pairs={{0,1},{1,2},{2,3},{4,5},{5,6},{6,7},{8,9},{9,10},{10,11},{12,13},{... | collective-permute-start | bytes 98312 | tf_op jit(solution)/shard_map/ppermute | solution.py:38
  10.9 11.6 %collective-permute-start.1 = (bf16[1,1,128,128]{3,2,1,0:T(8,128)(2,1)S(1)}, bf16[1,1,128,128]{3,2,1,0:T(8,128)(2,1)S(1)}, u32[]{:S(2)}, u32[]{:S(2)}) collective-permute-start(bf16[1,1,128,128]{3,2,1,0:T(8,128)(2,1)S(1)} %get-tuple-element.43), channel_id=1, source_target_pairs={{1,0},{2,1},{3,2},{5,4},{6,5},{7,6},{9,8},{10,9},{11,10},{13,12},{... | collective-permute-start | bytes 98312 | tf_op jit(solution)/shard_map/ppermute | solution.py:39
  13.0 14.4 %collective-permute-start.12 = (bf16[1,1,128,128]{3,2,1,0:T(8,128)(2,1)S(1)}, bf16[1,1,128,128]{3,2,1,0:T(8,128)(2,1)S(1)}, u32[]{:S(2)}, u32[]{:S(2)}) collective-permute-start(bf16[1,1,128,128]{3,2,1,0:T(8,128)(2,1)S(1)} %get-tuple-element.42), channel_id=1, source_target_pairs={{0,1},{1,2},{2,3},{4,5},{5,6},{6,7},{8,9},{9,10},{10,11},{12,13},{... | collective-permute-start | bytes 98312 | tf_op jit(solution)/shard_map/ppermute | solution.py:38
  18.2 9.9 %collective-permute-start.13 = (bf16[1,1,128,128]{3,2,1,0:T(8,128)(2,1)S(1)}, bf16[1,1,128,128]{3,2,1,0:T(8,128)(2,1)S(1)}, u32[]{:S(2)}, u32[]{:S(2)}) collective-permute-start(bf16[1,1,128,128]{3,2,1,0:T(8,128)(2,1)S(1)} %get-tuple-element.41), channel_id=1, source_target_pairs={{1,0},{2,1},{3,2},{5,4},{6,5},{7,6},{9,8},{10,9},{11,10},{13,12},{... | collective-permute-start | bytes 98312 | tf_op jit(solution)/shard_map/ppermute | solution.py:39
  22.7 11.4 %collective-permute-start.2 = (bf16[1,130,1,128]{3,2,1,0:T(2,128)(2,1)S(1)}, bf16[1,130,1,128]{3,2,1,0:T(2,128)(2,1)S(1)}, u32[]{:S(2)}, u32[]{:S(2)}) collective-permute-start(bf16[1,130,1,128]{3,2,1,0:T(2,128)(2,1)S(1)} %get-tuple-element.39), channel_id=1, source_target_pairs={{0,4},{4,8},{8,12},{1,5},{5,9},{9,13},{2,6},{6,10},{10,14},{3,7},{... | collective-permute-start | bytes 99848 | tf_op jit(solution)/shard_map/ppermute | solution.py:43
  26.1 7.9 %collective-permute-start.3 = (bf16[1,130,1,128]{3,2,1,0:T(2,128)(2,1)S(1)}, bf16[1,130,1,128]{3,2,1,0:T(2,128)(2,1)S(1)}, u32[]{:S(2)}, u32[]{:S(2)}) collective-permute-start(bf16[1,130,1,128]{3,2,1,0:T(2,128)(2,1)S(1)} %get-tuple-element.40), channel_id=1, source_target_pairs={{4,0},{8,4},{12,8},{5,1},{9,5},{13,9},{6,2},{10,6},{14,10},{7,3},{... | collective-permute-start | bytes 99848 | tf_op jit(solution)/shard_map/ppermute | solution.py:44
  28.0 6.0 %copy-start.13 = (bf16[1,130,128,128]{3,2,1,0:T(8,128)(2,1)}, bf16[1,130,128,128]{3,2,1,0:T(8,128)(2,1)S(1)}, u32[]{:S(2)}) copy-start(bf16[1,130,128,128]{3,2,1,0:T(8,128)(2,1)S(1)} %constant_dynamic-update-slice_fusion.5) | copy-start | bytes 12779524
  28.2 52.3 %collective-permute-start.14 = (bf16[1,130,1,128]{3,2,1,0:T(2,128)(2,1)S(1)}, bf16[1,130,1,128]{3,2,1,0:T(2,128)(2,1)S(1)}, u32[]{:S(2)}, u32[]{:S(2)}) collective-permute-start(bf16[1,130,1,128]{3,2,1,0:T(2,128)(2,1)S(1)} %get-tuple-element.37), channel_id=1, source_target_pairs={{0,4},{4,8},{8,12},{1,5},{5,9},{9,13},{2,6},{6,10},{10,14},{3,7},{... | collective-permute-start | bytes 99848 | tf_op jit(solution)/shard_map/ppermute | solution.py:43
  32.7 47.8 %collective-permute-start.15 = (bf16[1,130,1,128]{3,2,1,0:T(2,128)(2,1)S(1)}, bf16[1,130,1,128]{3,2,1,0:T(2,128)(2,1)S(1)}, u32[]{:S(2)}, u32[]{:S(2)}) collective-permute-start(bf16[1,130,1,128]{3,2,1,0:T(2,128)(2,1)S(1)} %get-tuple-element.38), channel_id=1, source_target_pairs={{4,0},{8,4},{12,8},{5,1},{9,5},{13,9},{6,2},{10,6},{14,10},{7,3},{... | collective-permute-start | bytes 99848 | tf_op jit(solution)/shard_map/ppermute | solution.py:44
  37.7 2.2 copy-start.2
  39.9 1.0 copy-start.23
  39.9 1.0 copy-start.25
  40.5 17.9 %copy-start.5 = (bf16[130,1,8,17,128]{4,2,3,0,1:T(8,128)(2,1)}, bf16[130,1,8,17,128]{4,2,3,0,1:T(8,128)(2,1)S(1)}, u32[]{:S(2)}) copy-start(bf16[130,1,8,17,128]{4,2,3,0,1:T(8,128)(2,1)S(1)} %copy.17) | copy-start | bytes 13578244
  58.5 15.7 %collective-permute-start.5 = (bf16[1,1,128,128]{3,1,2,0:T(2,128)(2,1)S(1)}, bf16[1,1,128,128]{3,1,2,0:T(2,128)(2,1)S(1)}, u32[]{:S(2)}, u32[]{:S(2)}) collective-permute-start(bf16[1,1,128,128]{3,1,2,0:T(2,128)(2,1)S(1)} %slice.155), channel_id=1, source_target_pairs={{1,0},{2,1},{3,2},{5,4},{6,5},{7,6},{9,8},{10,9},{11,10},{13,12},{... | collective-permute-start | bytes 98312 | tf_op jit(solution)/shard_map/ppermute | solution.py:39
  59.8 7.2 %slice-start.2 = ((bf16[130,1,8,17,128]{4,2,3,0,1:T(8,128)(2,1)}), bf16[130,1,8,16,128]{4,2,3,0,1:T(8,128)(2,1)S(1)}, s32[]{:S(2)}) async-start(bf16[130,1,8,17,128]{4,2,3,0,1:T(8,128)(2,1)} %copy-done.5), calls=%async_computation.3 | async-start | bytes 8519680 | tf_op jit(solution)/shard_map/concatenate | solution.py:45
  59.9 14.3 %collective-permute-start.4 = (bf16[1,1,128,128]{3,2,1,0:T(8,128)(2,1)S(1)}, bf16[1,1,128,128]{3,2,1,0:T(8,128)(2,1)S(1)}, u32[]{:S(2)}, u32[]{:S(2)}) collective-permute-start(bf16[1,1,128,128]{3,2,1,0:T(8,128)(2,1)S(1)} %slice.152), channel_id=1, source_target_pairs={{0,1},{1,2},{2,3},{4,5},{5,6},{6,7},{8,9},{9,10},{10,11},{12,13},{... | collective-permute-start | bytes 98312 | tf_op jit(solution)/shard_map/ppermute | solution.py:38
  71.0 9.5 %slice-start.4 = ((s8[4259840]{0:T(1024)(128)(4,1)}), s8[4194304]{0:T(1024)(128)(4,1)S(1)}, s32[]{:S(2)}) async-start(s8[4259840]{0:T(1024)(128)(4,1)} %bitcast.135), calls=%async_computation.5 | async-start | bytes 8388608
  71.0 9.5 %slice-start.5 = ((s8[4259840]{0:T(1024)(128)(4,1)}), s8[65536]{0:T(1024)(128)(4,1)S(1)}, s32[]{:S(2)}) async-start(s8[4259840]{0:T(1024)(128)(4,1)} %bitcast.135), calls=%async_computation.6 | async-start | bytes 131072
  74.2 14.4 %collective-permute-start.6 = (bf16[1,130,1,128]{3,1,2,0:T(8,128)(2,1)S(1)}, bf16[1,130,1,128]{3,1,2,0:T(8,128)(2,1)S(1)}, u32[]{:S(2)}, u32[]{:S(2)}) collective-permute-start(bf16[1,130,1,128]{3,1,2,0:T(8,128)(2,1)S(1)} %get-tuple-element.35), channel_id=1, source_target_pairs={{0,4},{4,8},{8,12},{1,5},{5,9},{9,13},{2,6},{6,10},{10,14},{3,7},{... | collective-permute-start | bytes 99848 | tf_op jit(solution)/shard_map/ppermute | solution.py:43
  79.2 9.5 %collective-permute-start.7 = (bf16[1,130,1,128]{3,1,2,0:T(8,128)(2,1)S(1)}, bf16[1,130,1,128]{3,1,2,0:T(8,128)(2,1)S(1)}, u32[]{:S(2)}, u32[]{:S(2)}) collective-permute-start(bf16[1,130,1,128]{3,1,2,0:T(8,128)(2,1)S(1)} %get-tuple-element.36), channel_id=1, source_target_pairs={{4,0},{8,4},{12,8},{5,1},{9,5},{13,9},{6,2},{10,6},{14,10},{7,3},{... | collective-permute-start | bytes 99848 | tf_op jit(solution)/shard_map/ppermute | solution.py:44
  83.4 2.2 slice-start
  84.2 1.7 slice-start.1
  94.0 2.3 copy-start.6
  96.2 14.0 %copy-start.21 = (bf16[3,3,128,128]{3,2,1,0:T(8,128)(2,1)S(1)}, bf16[3,3,128,128]{3,2,1,0:T(8,128)(2,1)}, u32[]{:S(2)}) copy-start(bf16[3,3,128,128]{3,2,1,0:T(8,128)(2,1)} %param.8) | copy-start | bytes 884740
  127.4 5.1 copy-start.14
  128.6 4.0 slice-start.3
  128.6 3.9 copy-start.17
  141.2 15.2 %copy-start.16 = (bf16[130,1,7,1,128]{4,2,3,0,1:T(8,128)(2,1)S(1)}, bf16[130,1,7,1,128]{4,2,3,0,1:T(8,128)(2,1)}, u32[]{:S(2)}) copy-start(bf16[130,1,7,1,128]{4,2,3,0,1:T(8,128)(2,1)} %get-tuple-element.18) | copy-start | bytes 698884
  144.2 47.8 %collective-permute-start.17 = (bf16[1,1,128,128]{3,1,2,0:T(2,128)(2,1)}, bf16[1,1,128,128]{3,1,2,0:T(2,128)(2,1)}, u32[]{:S(2)}, u32[]{:S(2)}) collective-permute-start(bf16[1,1,128,128]{3,1,2,0:T(2,128)(2,1)} %slice.173), channel_id=1, source_target_pairs={{1,0},{2,1},{3,2},{5,4},{6,5},{7,6},{9,8},{10,9},{11,10},{13,12},{... | collective-permute-start | bytes 98312 | tf_op jit(solution)/shard_map/ppermute | solution.py:39
  146.2 45.0 %collective-permute-start.16 = (bf16[1,1,128,128]{3,2,1,0:T(8,128)(2,1)}, bf16[1,1,128,128]{3,2,1,0:T(8,128)(2,1)}, u32[]{:S(2)}, u32[]{:S(2)}) collective-permute-start(bf16[1,1,128,128]{3,2,1,0:T(8,128)(2,1)} %slice.170), channel_id=1, source_target_pairs={{0,1},{1,2},{2,3},{4,5},{5,6},{6,7},{8,9},{9,10},{10,11},{12,13},{... | collective-permute-start | bytes 98312 | tf_op jit(solution)/shard_map/ppermute | solution.py:38
  152.3 47.3 %collective-permute-start.8 = (bf16[1,1,128,128]{3,0,2,1:T(2,128)(2,1)}, bf16[1,1,128,128]{3,0,2,1:T(2,128)(2,1)}, u32[]{:S(2)}, u32[]{:S(2)}) collective-permute-start(bf16[1,1,128,128]{3,0,2,1:T(2,128)(2,1)} %slice.158), channel_id=1, source_target_pairs={{0,1},{1,2},{2,3},{4,5},{5,6},{6,7},{8,9},{9,10},{10,11},{12,13},{... | collective-permute-start | bytes 98312 | tf_op jit(solution)/shard_map/ppermute | solution.py:38
  184.7 4.8 copy-start.18
  189.6 11.0 %copy-start.11 = (bf16[1,128,128,128]{3,1,2,0:T(8,128)(2,1)S(1)}, bf16[1,128,128,128]{3,1,2,0:T(8,128)(2,1)}, u32[]{:S(2)}) copy-start(bf16[1,128,128,128]{3,1,2,0:T(8,128)(2,1)} %slice_bitcast_fusion.4) | copy-start | bytes 12582916
  189.6 29.1 %collective-permute-start.9 = (bf16[1,1,128,128]{3,0,2,1:T(2,128)(2,1)S(1)}, bf16[1,1,128,128]{3,0,2,1:T(2,128)(2,1)S(1)}, u32[]{:S(2)}, u32[]{:S(2)}) collective-permute-start(bf16[1,1,128,128]{3,0,2,1:T(2,128)(2,1)S(1)} %slice.161), channel_id=1, source_target_pairs={{1,0},{2,1},{3,2},{5,4},{6,5},{7,6},{9,8},{10,9},{11,10},{13,12},{... | collective-permute-start | bytes 98312 | tf_op jit(solution)/shard_map/ppermute | solution.py:39
  192.9 32.6 %collective-permute-start.18 = (bf16[1,130,1,128]{3,1,2,0:T(8,128)(2,1)S(1)}, bf16[1,130,1,128]{3,1,2,0:T(8,128)(2,1)S(1)}, u32[]{:S(2)}, u32[]{:S(2)}) collective-permute-start(bf16[1,130,1,128]{3,1,2,0:T(8,128)(2,1)S(1)} %get-tuple-element.33), channel_id=1, source_target_pairs={{0,4},{4,8},{8,12},{1,5},{5,9},{9,13},{2,6},{6,10},{10,14},{3,7},{... | collective-permute-start | bytes 99848 | tf_op jit(solution)/shard_map/ppermute | solution.py:43
  198.3 27.2 %collective-permute-start.19 = (bf16[1,130,1,128]{3,1,2,0:T(8,128)(2,1)S(1)}, bf16[1,130,1,128]{3,1,2,0:T(8,128)(2,1)S(1)}, u32[]{:S(2)}, u32[]{:S(2)}) collective-permute-start(bf16[1,130,1,128]{3,1,2,0:T(8,128)(2,1)S(1)} %get-tuple-element.34), channel_id=1, source_target_pairs={{4,0},{8,4},{12,8},{5,1},{9,5},{13,9},{6,2},{10,6},{14,10},{7,3},{... | collective-permute-start | bytes 99848 | tf_op jit(solution)/shard_map/ppermute | solution.py:44
  200.5 24.9 %copy-start.3 = (bf16[1,128,128,128]{3,1,2,0:T(8,128)(2,1)S(1)}, bf16[1,128,128,128]{3,1,2,0:T(8,128)(2,1)}, u32[]{:S(2)}) copy-start(bf16[1,128,128,128]{3,1,2,0:T(8,128)(2,1)} %slice_bitcast_fusion.3) | copy-start | bytes 12582916
  218.8 6.7 %copy-start.12 = (bf16[1,130,128,128]{3,0,2,1:T(2,128)(2,1)}, bf16[1,130,128,128]{3,0,2,1:T(2,128)(2,1)S(1)}, u32[]{:S(2)}) copy-start(bf16[1,130,128,128]{3,0,2,1:T(2,128)(2,1)S(1)} %constant_dynamic-update-slice_fusion.3) | copy-start | bytes 12779524
  219.0 33.4 %collective-permute-start.10 = (bf16[1,130,1,128]{3,0,2,1:T(2,128)(2,1)S(1)}, bf16[1,130,1,128]{3,0,2,1:T(2,128)(2,1)S(1)}, u32[]{:S(2)}, u32[]{:S(2)}) collective-permute-start(bf16[1,130,1,128]{3,0,2,1:T(2,128)(2,1)S(1)} %get-tuple-element.13), channel_id=1, source_target_pairs={{0,4},{4,8},{8,12},{1,5},{5,9},{9,13},{2,6},{6,10},{10,14},{3,7},{... | collective-permute-start | bytes 99848 | tf_op jit(solution)/shard_map/ppermute | solution.py:43
  224.1 28.2 %collective-permute-start.11 = (bf16[1,130,1,128]{3,0,2,1:T(2,128)(2,1)S(1)}, bf16[1,130,1,128]{3,0,2,1:T(2,128)(2,1)S(1)}, u32[]{:S(2)}, u32[]{:S(2)}) collective-permute-start(bf16[1,130,1,128]{3,0,2,1:T(2,128)(2,1)S(1)} %get-tuple-element.14), channel_id=1, source_target_pairs={{4,0},{8,4},{12,8},{5,1},{9,5},{13,9},{6,2},{10,6},{14,10},{7,3},{... | collective-permute-start | bytes 99848 | tf_op jit(solution)/shard_map/ppermute | solution.py:44
  230.2 2.2 slice-start.6
  231.1 1.6 slice-start.7
  248.4 3.9 copy-start.15
  252.3 24.4 %copy-start.9 = (bf16[1,128,128,128]{3,2,1,0:T(8,128)(2,1)S(1)}, bf16[1,128,128,128]{3,2,1,0:T(8,128)(2,1)}, u32[]{:S(2)}) copy-start(bf16[1,128,128,128]{3,2,1,0:T(8,128)(2,1)} %param.9) | copy-start | bytes 12582916
  353.4 2.8 copy-start.20
  353.4 4.8 copy-start.19
  356.9 57.1 %collective-permute-start.21 = (bf16[1,1,128,128]{3,1,2,0:T(2,128)(2,1)}, bf16[1,1,128,128]{3,1,2,0:T(2,128)(2,1)}, u32[]{:S(2)}, u32[]{:S(2)}) collective-permute-start(bf16[1,1,128,128]{3,1,2,0:T(2,128)(2,1)} %slice.179), channel_id=1, source_target_pairs={{1,0},{2,1},{3,2},{5,4},{6,5},{7,6},{9,8},{10,9},{11,10},{13,12},{... | collective-permute-start | bytes 98312 | tf_op jit(solution)/shard_map/ppermute | solution.py:39
  358.9 54.2 %collective-permute-start.20 = (bf16[1,1,128,128]{3,2,1,0:T(8,128)(2,1)}, bf16[1,1,128,128]{3,2,1,0:T(8,128)(2,1)}, u32[]{:S(2)}, u32[]{:S(2)}) collective-permute-start(bf16[1,1,128,128]{3,2,1,0:T(8,128)(2,1)} %slice.176), channel_id=1, source_target_pairs={{0,1},{1,2},{2,3},{4,5},{5,6},{6,7},{8,9},{9,10},{10,11},{12,13},{... | collective-permute-start | bytes 98312 | tf_op jit(solution)/shard_map/ppermute | solution.py:38
  366.4 1.0 copy-start.22
  366.5 1.0 copy-start.26
  406.3 7.8 %copy-start.4 = (bf16[1,128,128,128]{3,1,2,0:T(8,128)(2,1)}, bf16[1,128,128,128]{3,1,2,0:T(8,128)(2,1)S(1)}, u32[]{:S(2)}) copy-start(bf16[1,128,128,128]{3,1,2,0:T(8,128)(2,1)S(1)} %slice_bitcast_fusion.2) | copy-start | bytes 12582916
  413.1 8.6 %copy-start.7 = (bf16[1,128,128,128]{3,2,1,0:T(8,128)(2,1)S(1)}, bf16[1,128,128,128]{3,2,1,0:T(8,128)(2,1)}, u32[]{:S(2)}) copy-start(bf16[1,128,128,128]{3,2,1,0:T(8,128)(2,1)} %param.5) | copy-start | bytes 12582916
  415.0 21.0 %collective-permute-start.22 = (bf16[1,130,1,128]{3,1,2,0:T(8,128)(2,1)S(1)}, bf16[1,130,1,128]{3,1,2,0:T(8,128)(2,1)S(1)}, u32[]{:S(2)}, u32[]{:S(2)}) collective-permute-start(bf16[1,130,1,128]{3,1,2,0:T(8,128)(2,1)S(1)} %get-tuple-element.31), channel_id=1, source_target_pairs={{0,4},{4,8},{8,12},{1,5},{5,9},{9,13},{2,6},{6,10},{10,14},{3,7},{... | collective-permute-start | bytes 99848 | tf_op jit(solution)/shard_map/ppermute | solution.py:43
  420.4 15.7 %collective-permute-start.23 = (bf16[1,130,1,128]{3,1,2,0:T(8,128)(2,1)S(1)}, bf16[1,130,1,128]{3,1,2,0:T(8,128)(2,1)S(1)}, u32[]{:S(2)}, u32[]{:S(2)}) collective-permute-start(bf16[1,130,1,128]{3,1,2,0:T(8,128)(2,1)S(1)} %get-tuple-element.32), channel_id=1, source_target_pairs={{4,0},{8,4},{12,8},{5,1},{9,5},{13,9},{6,2},{10,6},{14,10},{7,3},{... | collective-permute-start | bytes 99848 | tf_op jit(solution)/shard_map/ppermute | solution.py:44
  442.1 1.0 copy-start.24
  456.2 5.4 %copy-start.10 = (bf16[1,128,128,128]{3,2,1,0:T(8,128)(2,1)S(1)}, bf16[1,128,128,128]{3,2,1,0:T(8,128)(2,1)}, u32[]{:S(2)}) copy-start(bf16[1,128,128,128]{3,2,1,0:T(8,128)(2,1)} %param.9) | copy-start | bytes 12582916
  461.6 54.7 %copy-start.1 = (bf16[3,3,128,128]{3,2,1,0:T(8,128)(2,1)S(1)}, bf16[3,3,128,128]{3,2,1,0:T(8,128)(2,1)}, u32[]{:S(2)}) copy-start(bf16[3,3,128,128]{3,2,1,0:T(8,128)(2,1)} %param.7) | copy-start | bytes 884740
Sparse Core Ops, SparseCore 0:
  436.1 74.3 all-reduce.2
where the time goes:
time: 534 us; the launch traced here: 524 us
  matrix products  210 us (39%)
  local copies, waits for them, and re-layouts  115 us (22%)
  other arithmetic  77.6 us (15%)
  starting transfers between devices  70.6 us (13%)
  waiting for transfers between devices  34.4 us (6%)
  between operations  15.6 us (3%)
    conv_general_dilated x3, matrix products, weight_grad(): lax.conv_general_dilated(padded, grad, (1, 1), 'VALID', dimension_numbers...  123 us
    concatenate x10, other arithmetic, border_pad(): return jnp.concatenate([from_left, taller, from_right], axis=2)  56.4 us
    unnamed x81, local copies, waits for them, and re-layouts  50.4 us
    conv_general_dilated x3, matrix products, conv_back(): lax.conv_general_dilated(padded_grad, lax.rev(weight, (0, 1)), (1, 1), 'V...  46 us
    conv_general_dilated x3, matrix products, conv_valid(): lax.conv_general_dilated(padded, weight, (1, 1), 'VALID', dimension_numbe...  41.3 us
    psum x1, waiting for transfers between devices, local_block(): grad_w_first = lax.psum(weight_grad(img_pad, grad_pre1), ('row', 'col'))  34.3 us
    ppermute x6, starting transfers between devices, border_pad(): lax.ppermute(taller[:, :, taller.shape[2] - width:], 'col', right_pairs)  28.9 us
    ppermute x6, starting transfers between devices, border_pad(): lax.ppermute(tile[:, tile.shape[1] - width:], 'row', down_pairs)  25.9 us
  transfers between devices with their start and end apart: 25, of which 1 were waited for; matrix products, arithmetic and copies ran while one was open for 44% of the time, Pallas kernels for 0%

commit v1 on v0

v1 whole, which is shorter than its diff:
```python
import functools
import math
import jax
import jax.numpy as jnp
from jax import lax
from jax.experimental import pallas as pl
from jax.experimental.pallas import tpu as pltpu
from jax.sharding import PartitionSpec as P

GELU_SCALE = math.sqrt(2.0 / math.pi)
GELU_CUBIC = 0.044715
BF16 = jnp.bfloat16
F32 = jnp.float32

TILE = 128
CH = 128
ROW_HALO = 4
COL_HALO = 8
STRIPS = 16
STEPS = 9
PAD_STEPS = STEPS + 2
PAIRS = 68
FIRST_OWN = ROW_HALO // 2
OWN_PAIRS = TILE // 2
EXT_ROWS = TILE + 2 * ROW_HALO
EXT_COLS = TILE + 2 * COL_HALO
STAGE_ROWS = 8


def gelu_tanh(value):
    return 0.5 * value * (1.0 + jnp.tanh(GELU_SCALE * (value + GELU_CUBIC * value * value * value)))


def gelu_slope(value):
    tanh_val = jnp.tanh(GELU_SCALE * (value + GELU_CUBIC * value * value * value))
    return 0.5 * (1.0 + tanh_val) + 0.5 * value * (1.0 - tanh_val * tanh_val) * GELU_SCALE * (1.0 + 3.0 * GELU_CUBIC * value * value)


def row_at(ref, k, r, off):
    pair = k - 1 if r == 0 else k + 1 if r == 3 else k
    return pair + off, (r + 1) % 2


def pack_weights(w_ref, wp_ref, back):
    zero = jnp.zeros((CH, CH), BF16)
    for q in range(3):
        for p in range(3):
            if back:
                block = w_ref[2 - p, 2 - q].astype(F32).T.astype(BF16)
            else:
                block = w_ref[p, q]
            for b in range(2):
                wp_ref[pl.ds((q * 4 + p + b) * CH, CH), pl.ds(b * CH, CH)] = block
        wp_ref[pl.ds((q * 4 + 3) * CH, CH), pl.ds(0, CH)] = zero
        wp_ref[pl.ds((q * 4) * CH, CH), pl.ds(CH, CH)] = zero


def conv_stage(src, off, wp, first, count, per_step, epilogue):
    def body(step, carry):
        base = first + step * per_step
        for j in range(per_step):
            k = base + j
            parts = []
            for q in range(3):
                for r in range(4):
                    pair, par = row_at(src, k, r, off)
                    parts.append(src[pair, par, q:q + STEPS].reshape(STEPS * STRIPS, CH))
            acc = jnp.dot(jnp.concatenate(parts, axis=1), wp[...], preferred_element_type=F32)
            for par in range(2):
                epilogue(k, par, j, acc[:, par * CH:(par + 1) * CH].reshape(STEPS, STRIPS, CH))
        return carry
    lax.fori_loop(0, count // per_step, body, 0)


def with_edges(value):
    left = pltpu.roll(value[STEPS - 1], 1, 0)[None]
    right = pltpu.roll(value[0], STRIPS - 1, 0)[None]
    return jnp.concatenate([left, value, right], axis=0)


def wgrad_stage(val, off, grad, own_mask, acc, out, per_step):
    dims = (((0,), (0,)), ((), ()))
    flat = per_step * STEPS * STRIPS
    acc[...] = jnp.zeros_like(acc)

    def rows_of(k, r):
        pair, par = row_at(val, k, r, off)
        return val[pl.ds(pair, per_step), par, 1:1 + STEPS].reshape(flat, CH)

    def body(step, carry):
        k = FIRST_OWN + step * per_step
        rows = [rows_of(k, r) for r in range(4)]
        shifted = []
        for par in range(2):
            d = grad[pl.ds(k, per_step), par] * own_mask[...][None]
            shifted.append([d[:, 2 - q:2 - q + STEPS].reshape(flat, CH) for q in range(3)])
        lhs = jnp.concatenate([jnp.concatenate(rows[par:par + 3], axis=1) for par in range(2)], axis=0)
        rhs = jnp.concatenate([jnp.concatenate(shifted[par][:2], axis=1) for par in range(2)], axis=0)
        acc[:, 0:2 * CH] += lax.dot_general(lhs, rhs, dims, preferred_element_type=F32)
        both = jnp.concatenate([shifted[0][2], shifted[1][2]], axis=1)
        last = lax.dot_general(jnp.concatenate(rows, axis=1), both, dims, preferred_element_type=F32)
        acc[:, 2 * CH:3 * CH] += last[0:3 * CH, 0:CH] + last[CH:4 * CH, CH:2 * CH]
        return carry

    lax.fori_loop(0, OWN_PAIRS // per_step, body, 0)
    for p in range(3):
        for q in range(3):
            out[p, q] = acc[p * CH:(p + 1) * CH, q * CH:(q + 1) * CH]


def block_kernel(image, grad, w_first, w_second, w_third,
                 block_out, grad_image, dw_first, dw_second, dw_third,
                 xp, one, two, gp, d_two, d_one, a_one, a_two, wp,
                 stage, wide, outs, acc, img_mask, own_mask, in_sems, out_sems):
    row_id = lax.axis_index('row')
    col_id = lax.axis_index('col')
    n_rows, n_cols = 4, 4

    def load(src, b, slot):
        return pltpu.make_async_copy(src.at[pl.ds(b * STAGE_ROWS, STAGE_ROWS)], stage.at[slot], in_sems.at[slot])

    blocks = EXT_ROWS // STAGE_ROWS
    load(image, 0, 0).start()

    strip = lax.broadcasted_iota(jnp.int32, (PAD_STEPS, STRIPS, CH), 1)
    step = lax.broadcasted_iota(jnp.int32, (PAD_STEPS, STRIPS, CH), 0) - 1
    column = strip * STEPS + step
    own = (column >= COL_HALO) & (column < COL_HALO + TILE)
    own_mask[...] = own.astype(F32).astype(BF16)
    lowest = jnp.where(col_id == 0, COL_HALO, -1)
    highest = jnp.where(col_id == n_cols - 1, COL_HALO + TILE, EXT_COLS + 1)
    img_mask[...] = ((column >= lowest) & (column < highest)).astype(F32).astype(BF16)

    for i, (w_ref, back) in enumerate(((w_first, False), (w_second, False), (w_third, False), (w_third, True), (w_second, True), (w_first, True))):
        pack_weights(w_ref, wp.at[i], back)

    zero_row = jnp.zeros((PAD_STEPS, STRIPS, CH), BF16)
    xp[0, 1] = zero_row
    xp[PAIRS + 1, 0] = zero_row
    d_two[0, 1] = zero_row
    d_two[PAIRS - 1, 0] = zero_row
    wide[:, 0:8] = jnp.zeros((STAGE_ROWS, 8, CH), F32)
    wide[:, EXT_COLS + 8:EXT_COLS + 16] = jnp.zeros((STAGE_ROWS, 8, CH), F32)

    def to_strips(src, dst, off, nxt):
        def body(b, carry):
            slot = lax.rem(b, 2)

            @pl.when(b + 1 < blocks)
            def _():
                load(src, b + 1, 1 - slot).start()
            if nxt is not None:
                @pl.when(b + 1 == blocks)
                def _():
                    load(nxt, 0, 1 - slot).start()
            load(src, b, slot).wait()
            for r in range(STAGE_ROWS):
                wide[r, 8:8 + EXT_COLS] = stage[slot, r].astype(F32)
            for r in range(STAGE_ROWS):
                tiles = [wide[r, pl.ds(7 + t, STRIPS, stride=STEPS)] for t in range(PAD_STEPS)]
                dst[off + b * (STAGE_ROWS // 2) + r // 2, r % 2] = jnp.stack(tiles).astype(BF16)
            return carry
        return body

    lax.fori_loop(0, blocks, to_strips(image, xp, 1, None), 0)
    load(grad, 0, 0).start()
    lax.fori_loop(0, blocks, to_strips(grad, gp, 0, None), 0)

    def mask_rows(ref):
        zeros = jnp.zeros((2, 2, PAD_STEPS, STRIPS, CH), BF16)

        @pl.when(row_id == 0)
        def _():
            ref[0:2] = zeros

        @pl.when(row_id == n_rows - 1)
        def _():
            ref[PAIRS - 2:PAIRS] = zeros

    def forward_epilogue(pre, post):
        def epilogue(k, par, j, value):
            rounded = value.astype(BF16)
            pre[k, par] = rounded
            post[k, par] = with_edges(gelu_tanh(rounded.astype(F32))).astype(BF16) * img_mask[...]
        return epilogue

    def backward_epilogue(pre, post):
        def epilogue(k, par, j, value):
            slope = gelu_slope(pre[k, par].astype(F32))
            post[k, par] = with_edges(value * slope).astype(BF16) * img_mask[...]
        return epilogue

    conv_stage(xp, 1, wp.at[0], 0, PAIRS, 17, forward_epilogue(a_one, one))
    mask_rows(one)
    conv_stage(one, 0, wp.at[1], 1, PAIRS - 2, 11, forward_epilogue(a_two, two))
    mask_rows(two)
    conv_stage(gp, 0, wp.at[3], 1, PAIRS - 2, 11, backward_epilogue(a_two, d_two))
    mask_rows(d_two)
    wgrad_stage(two, 0, gp, own_mask, acc, dw_third, 16)
    conv_stage(d_two, 0, wp.at[4], 1, PAIRS - 2, 11, backward_epilogue(a_one, d_one))
    mask_rows(d_one)
    wgrad_stage(one, 0, d_two, own_mask, acc, dw_second, 16)
    wgrad_stage(xp, 1, d_one, own_mask, acc, dw_first, 16)

    per_out = 4
    out_steps = OWN_PAIRS // per_out

    def store(dst, s, slot):
        return pltpu.make_async_copy(outs.at[slot], dst.at[pl.ds(s * 2 * per_out, 2 * per_out)], out_sems.at[slot])

    def final_stage(src, wp_ref, skip, skip_off, dst):
        def body(s, carry):
            slot = lax.rem(s, 2)

            @pl.when(s >= 2)
            def _():
                store(dst, s - 2, slot).wait()
            base = FIRST_OWN + s * per_out
            for j in range(per_out):
                k = base + j
                parts = []
                for q in range(3):
                    for r in range(4):
                        pair, par = row_at(src, k, r, 0)
                        parts.append(src[pair, par, q:q + STEPS].reshape(STEPS * STRIPS, CH))
                res = jnp.dot(jnp.concatenate(parts, axis=1), wp_ref[...], preferred_element_type=F32)
                for par in range(2):
                    value = res[:, par * CH:(par + 1) * CH].reshape(STEPS, STRIPS, CH) + skip[k + skip_off, par, 1:1 + STEPS].astype(F32)
                    line = 2 * j + par
                    for t in range(STEPS):
                        wide[line, pl.ds(8 + t, STRIPS, stride=STEPS)] = value[t]
                    outs[slot, line] = wide[line, 8 + COL_HALO:8 + COL_HALO + TILE].astype(BF16)
            store(dst, s, slot).start()
            return carry
        lax.fori_loop(0, out_steps, body, 0)
        for s in range(out_steps - 2, out_steps):
            store(dst, s, s % 2).wait()

    final_stage(two, wp.at[2], xp, 1, block_out)
    final_stage(d_one, wp.at[5], gp, 0, grad_image)


def border_pad(tile, n_rows, n_cols):
    down_pairs = [(source, source + 1) for source in range(n_rows - 1)]
    up_pairs = [(source + 1, source) for source in range(n_rows - 1)]
    from_above = lax.ppermute(tile[tile.shape[0] - ROW_HALO:], 'row', down_pairs)
    from_below = lax.ppermute(tile[:ROW_HALO], 'row', up_pairs)
    taller = jnp.concatenate([from_above, tile, from_below], axis=0)
    right_pairs = [(source, source + 1) for source in range(n_cols - 1)]
    left_pairs = [(source + 1, source) for source in range(n_cols - 1)]
    from_left = lax.ppermute(taller[:, taller.shape[1] - COL_HALO:], 'col', right_pairs)
    from_right = lax.ppermute(taller[:, :COL_HALO], 'col', left_pairs)
    return jnp.concatenate([from_left, taller, from_right], axis=1)


def solution(mesh):
    n_rows = mesh.shape['row']
    n_cols = mesh.shape['col']
    act_spec = P(None, 'row', 'col', None)
    padded = (PAIRS, 2, PAD_STEPS, STRIPS, CH)
    plain = (PAIRS, 2, STEPS, STRIPS, CH)
    tile_shape = jax.ShapeDtypeStruct((TILE, TILE, CH), BF16)
    dw_shape = jax.ShapeDtypeStruct((3, 3, CH, CH), F32)
    hbm = pl.BlockSpec(memory_space=pl.ANY)
    vmem = pl.BlockSpec(memory_space=pltpu.VMEM)
    call = pl.pallas_call(
        block_kernel,
        out_shape=(tile_shape, tile_shape, dw_shape, dw_shape, dw_shape),
        in_specs=[hbm, hbm, vmem, vmem, vmem],
        out_specs=(hbm, hbm, vmem, vmem, vmem),
        scratch_shapes=[
            pltpu.VMEM((PAIRS + 2, 2, PAD_STEPS, STRIPS, CH), BF16),
            pltpu.VMEM(padded, BF16), pltpu.VMEM(padded, BF16), pltpu.VMEM(padded, BF16),
            pltpu.VMEM(padded, BF16), pltpu.VMEM(padded, BF16),
            pltpu.VMEM(plain, BF16), pltpu.VMEM(plain, BF16),
            pltpu.VMEM((6, 12 * CH, 2 * CH), BF16),
            pltpu.VMEM((2, STAGE_ROWS, EXT_COLS, CH), BF16),
            pltpu.VMEM((STAGE_ROWS, EXT_COLS + 16, CH), F32),
            pltpu.VMEM((2, 8, TILE, CH), BF16),
            pltpu.VMEM((3 * CH, 3 * CH), F32),
            pltpu.VMEM((PAD_STEPS, STRIPS, CH), BF16),
            pltpu.VMEM((PAD_STEPS, STRIPS, CH), BF16),
            pltpu.SemaphoreType.DMA((2,)),
            pltpu.SemaphoreType.DMA((2,)),
        ],
        compiler_params=pltpu.CompilerParams(vmem_limit_bytes=67043328),
        name='block',
    )

    def local_block(image, w_first, w_second, w_third, grad_out):
        image_ext = border_pad(image[0], n_rows, n_cols)
        grad_ext = border_pad(grad_out[0], n_rows, n_cols)
        out, dx, dw1, dw2, dw3 = call(image_ext, grad_ext, w_first, w_second, w_third)
        dw1, dw2, dw3 = lax.psum((dw1, dw2, dw3), ('row', 'col'))
        return out[None], dx[None], dw1, dw2, dw3

    return jax.shard_map(local_block, mesh=mesh, in_specs=(act_spec, P(), P(), P(), act_spec), out_specs=(act_spec, act_spec, P(), P(), P()), check_vma=False)
```

time: 534 us -> 248 us (0.46); the launches traced: 524 us -> 247 us
  matrix products: 210 us -> 0 us
  Pallas kernels: 0 us -> 109 us
  local copies, waits for them, and re-layouts: 115 us -> 6.91 us
  other arithmetic: 77.6 us -> 12.3 us
  starting transfers between devices: 70.6 us -> 21 us
  waiting for transfers between devices: 34.4 us -> 83.4 us
    conv_general_dilated x9 -> x0, matrix products: 210 us -> none  [the longest x3 123 us: weight_grad(): lax.conv_general_dilated(padded, grad, (1, 1), 'VALID', dimension_numbers...]
    pallas_call x0 -> x1, Pallas kernels: none -> 109 us  [local_block(): call(image_ext, grad_ext, w_first, w_second, w_third)]
    ppermute x24 -> x8, starting transfers between devices: 70.6 us -> 21 us  [the longest x2 7.96 us: border_pad(): lax.ppermute(tile[tile.shape[0] - ROW_HALO:], 'row', down_pairs)]
    concatenate x10 -> x2, other arithmetic: 56.4 us -> 11 us  [border_pad(): return jnp.concatenate([from_left, taller, from_right], axis=1)]
    unnamed x81 -> x7, local copies, waits for them, and re-layouts: 50.4 us -> 5.76 us
    psum x1, waiting for transfers between devices: 34.3 us -> 71.2 us  [local_block(): dw1, dw2, dw3 = lax.psum((dw1, dw2, dw3), ('row', 'col'))]
    convert_element_type x36 -> x0, local copies, waits for them, and re-layouts: 28.2 us -> none  [the longest x9 9.55 us: forward_acts(): gelu_tanh(pre_two.astype(jnp.float32)).astype(jnp.bfloat16)]
    convert_element_type x2 -> x0, other arithmetic: 19.4 us -> none  [the longest x1 9.85 us: local_block(): (conv_back(pre1_pad, w_first) + grad_out.astype(jnp.float32)).astype(jnp....]
  transfers between devices with their start and end apart: 25 -> 9, of which waited for: 1 -> 4; matrix products, arithmetic and copies ran while one was open for 44% -> 2% of each run, Pallas kernels for 0% -> 0%
where the time goes in v1:
time: 248 us; the launch traced here: 247 us
  Pallas kernels  109 us (44%)
  waiting for transfers between devices  83.4 us (34%)
  starting transfers between devices  21 us (8%)
  between operations  14.2 us (6%)
  other arithmetic  12.3 us (5%)
  local copies, waits for them, and re-layouts  6.91 us (3%)
    pallas_call x1, Pallas kernels, local_block(): call(image_ext, grad_ext, w_first, w_second, w_third)  109 us
    psum x1, waiting for transfers between devices, local_block(): dw1, dw2, dw3 = lax.psum((dw1, dw2, dw3), ('row', 'col'))  71.2 us
    concatenate x2, other arithmetic, border_pad(): return jnp.concatenate([from_left, taller, from_right], axis=1)  11 us
    ppermute x2, starting transfers between devices, border_pad(): lax.ppermute(tile[tile.shape[0] - ROW_HALO:], 'row', down_pairs)  7.96 us
    ppermute x2, starting transfers between devices, border_pad(): lax.ppermute(taller[:, taller.shape[1] - COL_HALO:], 'col', right_pairs)  7.86 us
    ppermute x2, waiting for transfers between devices, border_pad(): from_right = lax.ppermute(taller[:, :COL_HALO], 'col', left_pairs)  6.2 us
    ppermute x2, waiting for transfers between devices, border_pad(): from_below = lax.ppermute(tile[:ROW_HALO], 'row', up_pairs)  5.96 us
    unnamed x7, local copies, waits for them, and re-layouts  5.76 us
  transfers between devices with their start and end apart: 9, of which 4 were waited for; matrix products, arithmetic and copies ran while one was open for 2% of the time, Pallas kernels for 0%

profile of v1, /device:TPU:0, one launch (start us, length us, event | category | flops | bytes accessed | tf_op | source)
XLA Modules:
  0.0 247.0 jit_solution(15308075930351394704)
XLA Ops:
  7.2 0.0 all-reduce.3.cloned.1.call-start
  7.2 0.0 copy-start.1
  7.2 1.1 slice_bitcast_fusion.3
  8.4 2.8 %collective-permute-start = (bf16[4,128,128]{2,1,0:T(8,128)(2,1)S(1)}, bf16[4,128,128]{2,1,0:T(8,128)(2,1)S(1)}, u32[]{:S(2)}, u32[]{:S(2)}) collective-permute-start(bf16[4,128,128]{2,1,0:T(8,128)(2,1)S(1)} %get-tuple-element.24), channel_id=1, source_target_pairs={{0,1},{1,2},{2,3},{4,5},{5,6},{6,7},{8,9},{9,10},{10,11},{12,13},{... | collective-permute-start | bytes 393224 | tf_op jit(solution)/shard_map/ppermute | solution.py:246
  11.2 1.3 collective-permute-start.1
  12.5 0.0 collective-permute-done
  12.5 4.0 %collective-permute-done.1 = bf16[4,128,128]{2,1,0:T(8,128)(2,1)S(1)} collective-permute-done((bf16[4,128,128]{2,1,0:T(8,128)(2,1)S(1)}, bf16[4,128,128]{2,1,0:T(8,128)(2,1)S(1)}, u32[]{:S(2)}, u32[]{:S(2)}) %collective-permute-start.1) | collective-permute-done | bytes 131104 | tf_op jit(solution)/shard_map/ppermute | solution.py:247
  16.5 0.0 copy-start
  16.5 1.2 pad_maximum_fusion.7
  17.7 3.6 %collective-permute-start.2 = (bf16[136,8,128]{2,1,0:T(8,128)(2,1)S(1)}, bf16[136,8,128]{2,1,0:T(8,128)(2,1)S(1)}, u32[]{:S(2)}, u32[]{:S(2)}) collective-permute-start(bf16[136,8,128]{2,1,0:T(8,128)(2,1)S(1)} %get-tuple-element.20), channel_id=1, source_target_pairs={{0,4},{4,8},{8,12},{1,5},{5,9},{9,13},{2,6},{6,10},{10,14},{3,7},{... | collective-permute-start | bytes 835592 | tf_op jit(solution)/shard_map/ppermute | solution.py:251
  21.3 1.3 collective-permute-start.3
  22.6 0.0 copy-done.1
  22.6 5.2 %collective-permute-start.4 = (bf16[4,128,128]{2,1,0:T(8,128)(2,1)S(1)}, bf16[4,128,128]{2,1,0:T(8,128)(2,1)S(1)}, u32[]{:S(2)}, u32[]{:S(2)}) collective-permute-start(bf16[4,128,128]{2,1,0:T(8,128)(2,1)S(1)} %get-tuple-element.22), channel_id=1, source_target_pairs={{0,1},{1,2},{2,3},{4,5},{5,6},{6,7},{8,9},{9,10},{10,11},{12,13},{... | collective-permute-start | bytes 393224 | tf_op jit(solution)/shard_map/ppermute | solution.py:246
  27.8 1.3 collective-permute-start.5
  29.1 0.0 collective-permute-done.4
  29.1 1.9 collective-permute-done.5
  31.1 0.1 pad_maximum_fusion.4
  31.2 4.3 %collective-permute-start.6 = (bf16[136,8,128]{2,1,0:T(8,128)(2,1)S(1)}, bf16[136,8,128]{2,1,0:T(8,128)(2,1)S(1)}, u32[]{:S(2)}, u32[]{:S(2)}) collective-permute-start(bf16[136,8,128]{2,1,0:T(8,128)(2,1)S(1)} %get-tuple-element.18), channel_id=1, source_target_pairs={{0,4},{4,8},{8,12},{1,5},{5,9},{9,13},{2,6},{6,10},{10,14},{3,7},{... | collective-permute-start | bytes 835592 | tf_op jit(solution)/shard_map/ppermute | solution.py:251
  35.4 1.3 collective-permute-start.7
  36.7 0.0 collective-permute-done.2
  36.8 0.0 collective-permute-done.3
  36.8 0.0 copy-done
  36.8 5.5 %pad_maximum_fusion.image = bf16[136,144,128]{2,1,0:T(8,128)(2,1)} fusion(bf16[136,8,128]{2,1,0:T(8,128)(2,1)S(1)} %collective-permute-done.3, bf16[4,128,128]{2,1,0:T(8,128)(2,1)S(1)} %collective-permute-done.1, bf16[128,128,128]{2,1,0:T(8,128)(2,1)S(1)} %bitcast.13, bf16[4,128,128]{2,1,0:T(8,128)(2,1)S(1)} %collective-permute-done, ...), kind=kLoop, calls=%fused_computation | loop fusion | flops 25067520 | bytes 10027008 | tf_op jit(solution)/shard_map/concatenate | solution.py:253
  42.3 0.0 collective-permute-done.6
  42.3 6.2 %collective-permute-done.7 = bf16[136,8,128]{2,1,0:T(8,128)(2,1)S(1)} collective-permute-done((bf16[136,8,128]{2,1,0:T(8,128)(2,1)S(1)}, bf16[136,8,128]{2,1,0:T(8,128)(2,1)S(1)}, u32[]{:S(2)}, u32[]{:S(2)}) %collective-permute-start.7) | collective-permute-done | bytes 278560 | tf_op jit(solution)/shard_map/ppermute | solution.py:252
  48.5 5.6 %pad_maximum_fusion.1.grad = bf16[136,144,128]{2,1,0:T(8,128)(2,1)} fusion(bf16[136,8,128]{2,1,0:T(8,128)(2,1)S(1)} %collective-permute-done.7, bf16[4,128,128]{2,1,0:T(8,128)(2,1)S(1)} %collective-permute-done.5, bf16[128,128,128]{2,1,0:T(8,128)(2,1)S(1)} %bitcast.15, bf16[4,128,128]{2,1,0:T(8,128)(2,1)S(1)} %collective-permute-done.4, ...), kind=kLoop, calls=%fused_computation.1 | loop fusion | flops 25067520 | bytes 10027008 | tf_op jit(solution)/shard_map/concatenate | solution.py:253
  54.0 109.2 %block.1 = (bf16[128,128,128]{2,1,0:T(8,128)(2,1)}, bf16[128,128,128]{2,1,0:T(8,128)(2,1)}, f32[3,3,128,128]{3,2,1,0:T(8,128)}, f32[3,3,128,128]{3,2,1,0:T(8,128)}, f32[3,3,128,128]{3,2,1,0:T(8,128)}) custom-call(bf16[136,144,128]{2,1,0:T(8,128)(2,1)} %pad_maximum_fusion.image, bf16[136,144,128]{2,1,0:T(8,128)(2,1)} %pad_maximum_fusion.1.grad, ...), custom_call_target="tpu_custom_call" | custom-call | tf_op jit(solution)/shard_map/block/pallas_call | solution.py:293
  163.2 0.0 all-reduce.3.cloned.1.call-update
  163.2 71.2 %all-reduce.3.cloned.1.call-done = (f32[3,3,128,128]{3,2,1,0:T(8,128)}, f32[3,3,128,128]{3,2,1,0:T(8,128)}, f32[3,3,128,128]{3,2,1,0:T(8,128)}) async-done(((f32[3,3,128,128]{3,2,1,0:T(8,128)}, f32[3,3,128,128]{3,2,1,0:T(8,128)}, f32[3,3,128,128]{3,2,1,0:T(8,128)}), (f32[3,3,128,128]{3,2,1,0:T(8,128)}, f32[3,3,128,128]{3,2,1,0:T(8,128)}, f32[3,3,128,128]{3,2,1,0:T(8,128)})) %all-reduce.3.cloned.1.call-update) | async-done | bytes 1769488 | tf_op jit(solution)/shard_map/psum | solution.py:294
  234.4 1.9 copy.13
  236.3 1.9 copy.14
  238.3 1.9 copy.15
  (1 shorter events, 0.0 us)
Async XLA Ops:
  7.2 227.3 %all-reduce.3.cloned.1.call-start = ((), (), s32[]{:S(2)}) async-start(), calls=%async_computation | async-start | bytes 3538944 | tf_op jit(solution)/shard_map/psum | solution.py:294
  7.2 15.4 %copy-start.1 = (bf16[1,128,128,128]{3,2,1,0:T(8,128)(2,1)S(1)}, bf16[1,128,128,128]{3,2,1,0:T(8,128)(2,1)}, u32[]{:S(2)}) copy-start(bf16[1,128,128,128]{3,2,1,0:T(8,128)(2,1)} %param.9) | copy-start | bytes 12582916
  8.4 4.1 %collective-permute-start = (bf16[4,128,128]{2,1,0:T(8,128)(2,1)S(1)}, bf16[4,128,128]{2,1,0:T(8,128)(2,1)S(1)}, u32[]{:S(2)}, u32[]{:S(2)}) collective-permute-start(bf16[4,128,128]{2,1,0:T(8,128)(2,1)S(1)} %get-tuple-element.24), channel_id=1, source_target_pairs={{0,1},{1,2},{2,3},{4,5},{5,6},{6,7},{8,9},{9,10},{10,11},{12,13},{... | collective-permute-start | bytes 393224 | tf_op jit(solution)/shard_map/ppermute | solution.py:246
  11.2 5.3 %collective-permute-start.1 = (bf16[4,128,128]{2,1,0:T(8,128)(2,1)S(1)}, bf16[4,128,128]{2,1,0:T(8,128)(2,1)S(1)}, u32[]{:S(2)}, u32[]{:S(2)}) collective-permute-start(bf16[4,128,128]{2,1,0:T(8,128)(2,1)S(1)} %get-tuple-element.25), channel_id=1, source_target_pairs={{1,0},{2,1},{3,2},{5,4},{6,5},{7,6},{9,8},{10,9},{11,10},{13,12},{... | collective-permute-start | bytes 393224 | tf_op jit(solution)/shard_map/ppermute | solution.py:247
  16.5 20.3 %copy-start = (bf16[1,128,128,128]{3,2,1,0:T(8,128)(2,1)S(1)}, bf16[1,128,128,128]{3,2,1,0:T(8,128)(2,1)}, u32[]{:S(2)}) copy-start(bf16[1,128,128,128]{3,2,1,0:T(8,128)(2,1)} %param.5) | copy-start | bytes 12582916
  17.7 19.0 %collective-permute-start.2 = (bf16[136,8,128]{2,1,0:T(8,128)(2,1)S(1)}, bf16[136,8,128]{2,1,0:T(8,128)(2,1)S(1)}, u32[]{:S(2)}, u32[]{:S(2)}) collective-permute-start(bf16[136,8,128]{2,1,0:T(8,128)(2,1)S(1)} %get-tuple-element.20), channel_id=1, source_target_pairs={{0,4},{4,8},{8,12},{1,5},{5,9},{9,13},{2,6},{6,10},{10,14},{3,7},{... | collective-permute-start | bytes 835592 | tf_op jit(solution)/shard_map/ppermute | solution.py:251
  21.3 15.4 %collective-permute-start.3 = (bf16[136,8,128]{2,1,0:T(8,128)(2,1)S(1)}, bf16[136,8,128]{2,1,0:T(8,128)(2,1)S(1)}, u32[]{:S(2)}, u32[]{:S(2)}) collective-permute-start(bf16[136,8,128]{2,1,0:T(8,128)(2,1)S(1)} %get-tuple-element.21), channel_id=1, source_target_pairs={{4,0},{8,4},{12,8},{5,1},{9,5},{13,9},{6,2},{10,6},{14,10},{7,3},{... | collective-permute-start | bytes 835592 | tf_op jit(solution)/shard_map/ppermute | solution.py:252
  22.6 6.5 %collective-permute-start.4 = (bf16[4,128,128]{2,1,0:T(8,128)(2,1)S(1)}, bf16[4,128,128]{2,1,0:T(8,128)(2,1)S(1)}, u32[]{:S(2)}, u32[]{:S(2)}) collective-permute-start(bf16[4,128,128]{2,1,0:T(8,128)(2,1)S(1)} %get-tuple-element.22), channel_id=1, source_target_pairs={{0,1},{1,2},{2,3},{4,5},{5,6},{6,7},{8,9},{9,10},{10,11},{12,13},{... | collective-permute-start | bytes 393224 | tf_op jit(solution)/shard_map/ppermute | solution.py:246
  27.8 3.2 %collective-permute-start.5 = (bf16[4,128,128]{2,1,0:T(8,128)(2,1)S(1)}, bf16[4,128,128]{2,1,0:T(8,128)(2,1)S(1)}, u32[]{:S(2)}, u32[]{:S(2)}) collective-permute-start(bf16[4,128,128]{2,1,0:T(8,128)(2,1)S(1)} %get-tuple-element.23), channel_id=1, source_target_pairs={{1,0},{2,1},{3,2},{5,4},{6,5},{7,6},{9,8},{10,9},{11,10},{13,12},{... | collective-permute-start | bytes 393224 | tf_op jit(solution)/shard_map/ppermute | solution.py:247
  31.2 11.1 %collective-permute-start.6 = (bf16[136,8,128]{2,1,0:T(8,128)(2,1)S(1)}, bf16[136,8,128]{2,1,0:T(8,128)(2,1)S(1)}, u32[]{:S(2)}, u32[]{:S(2)}) collective-permute-start(bf16[136,8,128]{2,1,0:T(8,128)(2,1)S(1)} %get-tuple-element.18), channel_id=1, source_target_pairs={{0,4},{4,8},{8,12},{1,5},{5,9},{9,13},{2,6},{6,10},{10,14},{3,7},{... | collective-permute-start | bytes 835592 | tf_op jit(solution)/shard_map/ppermute | solution.py:251
  35.4 13.0 %collective-permute-start.7 = (bf16[136,8,128]{2,1,0:T(8,128)(2,1)S(1)}, bf16[136,8,128]{2,1,0:T(8,128)(2,1)S(1)}, u32[]{:S(2)}, u32[]{:S(2)}) collective-permute-start(bf16[136,8,128]{2,1,0:T(8,128)(2,1)S(1)} %get-tuple-element.19), channel_id=1, source_target_pairs={{4,0},{8,4},{12,8},{5,1},{9,5},{13,9},{6,2},{10,6},{14,10},{7,3},{... | collective-permute-start | bytes 835592 | tf_op jit(solution)/shard_map/ppermute | solution.py:252
Sparse Core Ops, SparseCore 0:
  163.4 71.0 all-reduce.2

commit v2 on v1

--- a/solution.py
+++ b/solution.py
@@ -25,6 +25,10 @@
 EXT_ROWS = TILE + 2 * ROW_HALO
 EXT_COLS = TILE + 2 * COL_HALO
 STAGE_ROWS = 8
+QUAD = 4
+N_ROWS = 4
+N_COLS = 4
+CHUNK = 9 * CH // (N_ROWS * N_COLS)
 
 
 def gelu_tanh(value):
@@ -105,22 +109,41 @@
     lax.fori_loop(0, OWN_PAIRS // per_step, body, 0)
     for p in range(3):
         for q in range(3):
-            out[p, q] = acc[p * CH:(p + 1) * CH, q * CH:(q + 1) * CH]
-
-
-def block_kernel(image, grad, w_first, w_second, w_third,
+            out[(p * 3 + q) * CH:(p * 3 + q + 1) * CH] = acc[p * CH:(p + 1) * CH, q * CH:(q + 1) * CH]
+
+
+def directions():
+    return [(dr, dc) for dr in (-1, 0, 1) for dc in (-1, 0, 1) if (dr, dc) != (0, 0)]
+
+
+def block_kernel(image, image_quads, image_pairs, grad, grad_quads, grad_pairs, w_first, w_second, w_third,
                  block_out, grad_image, dw_first, dw_second, dw_third,
                  xp, one, two, gp, d_two, d_one, a_one, a_two, wp,
-                 stage, wide, outs, acc, img_mask, own_mask, in_sems, out_sems):
+                 halo, wide, outs, acc, img_mask, own_mask, part, got, final,
+                 in_sems, out_sems, halo_send, halo_recv, sum_send, sum_recv, all_send, all_recv):
+    n_rows, n_cols = N_ROWS, N_COLS
+    n_dev = n_rows * n_cols
     row_id = lax.axis_index('row')
     col_id = lax.axis_index('col')
-    n_rows, n_cols = 4, 4
-
-    def load(src, b, slot):
-        return pltpu.make_async_copy(src.at[pl.ds(b * STAGE_ROWS, STAGE_ROWS)], stage.at[slot], in_sems.at[slot])
-
-    blocks = EXT_ROWS // STAGE_ROWS
-    load(image, 0, 0).start()
+    me = col_id * n_rows + row_id
+
+    def local(i):
+        src, dst = ((image_pairs, d_one), (grad_pairs, d_two))[i]
+        return pltpu.make_async_copy(src, dst.at[pl.ds(FIRST_OWN, OWN_PAIRS), :, pl.ds(0, 8)], in_sems.at[i])
+
+    local(0).start()
+    local(1).start()
+
+    barrier = pltpu.get_barrier_semaphore()
+
+    def device(d):
+        other = lax.rem(me + d, n_dev)
+        return other, {'col': other // n_rows, 'row': lax.rem(other, n_rows)}
+
+    def greet(d, carry):
+        pl.semaphore_signal(barrier, inc=1, device_id=device(d)[1], device_id_type=pl.DeviceIdType.MESH)
+        return carry
+    lax.fori_loop(1, n_dev, greet, 0)
 
     strip = lax.broadcasted_iota(jnp.int32, (PAD_STEPS, STRIPS, CH), 1)
     step = lax.broadcasted_iota(jnp.int32, (PAD_STEPS, STRIPS, CH), 0) - 1
@@ -130,52 +153,89 @@
     lowest = jnp.where(col_id == 0, COL_HALO, -1)
     highest = jnp.where(col_id == n_cols - 1, COL_HALO + TILE, EXT_COLS + 1)
     img_mask[...] = ((column >= lowest) & (column < highest)).astype(F32).astype(BF16)
-
-    for i, (w_ref, back) in enumerate(((w_first, False), (w_second, False), (w_third, False), (w_third, True), (w_second, True), (w_first, True))):
-        pack_weights(w_ref, wp.at[i], back)
-
     zero_row = jnp.zeros((PAD_STEPS, STRIPS, CH), BF16)
     xp[0, 1] = zero_row
     xp[PAIRS + 1, 0] = zero_row
-    d_two[0, 1] = zero_row
-    d_two[PAIRS - 1, 0] = zero_row
-    wide[:, 0:8] = jnp.zeros((STAGE_ROWS, 8, CH), F32)
-    wide[:, EXT_COLS + 8:EXT_COLS + 16] = jnp.zeros((STAGE_ROWS, 8, CH), F32)
-
-    def to_strips(src, dst, off, nxt):
-        def body(b, carry):
-            slot = lax.rem(b, 2)
-
-            @pl.when(b + 1 < blocks)
+    wide[:, 0:16] = jnp.zeros((STAGE_ROWS, 16, CH), F32)
+    wide[:, TILE + 16:TILE + 32] = jnp.zeros((STAGE_ROWS, 16, CH), F32)
+
+    @pl.when(col_id == 0)
+    def _():
+        halo[0, 0] = jnp.zeros((EXT_ROWS, QUAD, CH), BF16)
+        halo[1, 0] = jnp.zeros((EXT_ROWS, QUAD, CH), BF16)
+
+    @pl.when(col_id == n_cols - 1)
+    def _():
+        halo[0, 1] = jnp.zeros((EXT_ROWS, QUAD, CH), BF16)
+        halo[1, 1] = jnp.zeros((EXT_ROWS, QUAD, CH), BF16)
+
+    pl.semaphore_wait(barrier, n_dev - 1)
+
+    def halo_copy(i, n, dr, dc):
+        quads, pairs, natural = ((image_quads, image_pairs, d_one), (grad_quads, grad_pairs, d_two))[i]
+        if dc == 0:
+            src = pairs.at[pl.ds(0, 2)] if dr < 0 else pairs.at[pl.ds(OWN_PAIRS - 2, 2)]
+            dst = natural.at[pl.ds(PAIRS - 2, 2) if dr < 0 else pl.ds(0, 2), :, pl.ds(0, 8)]
+        else:
+            rows = (pl.ds(0, ROW_HALO), pl.ds(0, TILE), pl.ds(TILE - ROW_HALO, ROW_HALO))[dr + 1]
+            into = (pl.ds(EXT_ROWS - ROW_HALO, ROW_HALO), pl.ds(ROW_HALO, TILE), pl.ds(0, ROW_HALO))[dr + 1]
+            src = quads.at[rows, 0 if dc < 0 else TILE // QUAD - 1]
+            dst = halo.at[i, 1 if dc < 0 else 0, into]
+        return pltpu.make_async_remote_copy(
+            src_ref=src, dst_ref=dst, send_sem=halo_send.at[i, n], recv_sem=halo_recv.at[i, n],
+            device_id={'col': col_id + dc, 'row': row_id + dr}, device_id_type=pl.DeviceIdType.MESH)
+
+    def exists(dr, dc):
+        ok = None
+        for pos, shift, size in ((row_id, dr, n_rows), (col_id, dc, n_cols)):
+            if shift:
+                one_ok = (pos + shift >= 0) & (pos + shift < size)
+                ok = one_ok if ok is None else ok & one_ok
+        return ok
+
+    for i in range(2):
+        for n, (dr, dc) in enumerate(directions()):
+            @pl.when(exists(dr, dc))
             def _():
-                load(src, b + 1, 1 - slot).start()
-            if nxt is not None:
-                @pl.when(b + 1 == blocks)
-                def _():
-                    load(nxt, 0, 1 - slot).start()
-            load(src, b, slot).wait()
-            for r in range(STAGE_ROWS):
-                wide[r, 8:8 + EXT_COLS] = stage[slot, r].astype(F32)
-            for r in range(STAGE_ROWS):
-                tiles = [wide[r, pl.ds(7 + t, STRIPS, stride=STEPS)] for t in range(PAD_STEPS)]
-                dst[off + b * (STAGE_ROWS // 2) + r // 2, r % 2] = jnp.stack(tiles).astype(BF16)
-            return carry
-        return body
-
-    lax.fori_loop(0, blocks, to_strips(image, xp, 1, None), 0)
-    load(grad, 0, 0).start()
-    lax.fori_loop(0, blocks, to_strips(grad, gp, 0, None), 0)
-
-    def mask_rows(ref):
+                halo_copy(i, n, dr, dc).start()
+
+    for i, (w_ref, back) in enumerate(((w_first, False), (w_second, False), (w_third, False), (w_third, True), (w_second, True), (w_first, True))):
+        pack_weights(w_ref, wp.at[i], back)
+
+    def halo_wait(i):
+        for n, (dr, dc) in enumerate(directions()):
+            @pl.when(exists(-dr, -dc))
+            def _():
+                halo_copy(i, n, dr, dc).wait_recv()
+
+    def mask_rows(ref, off=0):
         zeros = jnp.zeros((2, 2, PAD_STEPS, STRIPS, CH), BF16)
 
         @pl.when(row_id == 0)
         def _():
-            ref[0:2] = zeros
+            ref[off:off + 2] = zeros
 
         @pl.when(row_id == n_rows - 1)
         def _():
-            ref[PAIRS - 2:PAIRS] = zeros
+            ref[off + PAIRS - 2:off + PAIRS] = zeros
+
+    def to_strips(i, natural, dst, off):
+        local(i).wait()
+        halo_wait(i)
+
+        def body(b, carry):
+            for r in range(STAGE_ROWS):
+                k, par = b * (STAGE_ROWS // 2) + r // 2, r % 2
+                wide[r, 16:16 + TILE] = natural[k, par, 0:8].reshape(TILE, CH).astype(F32)
+                wide[r, 16 - QUAD:16] = halo[i, 0, 2 * k + par].astype(F32)
+                wide[r, 16 + TILE:16 + TILE + QUAD] = halo[i, 1, 2 * k + par].astype(F32)
+            for r in range(STAGE_ROWS):
+                k, par = b * (STAGE_ROWS // 2) + r // 2, r % 2
+                tiles = [wide[r, pl.ds(7 + t, STRIPS, stride=STEPS)] for t in range(PAD_STEPS)]
+                dst[off + k, par] = jnp.stack(tiles).astype(BF16)
+            return carry
+        lax.fori_loop(0, EXT_ROWS // STAGE_ROWS, body, 0)
+        mask_rows(dst, off)
 
     def forward_epilogue(pre, post):
         def epilogue(k, par, j, value):
@@ -190,17 +250,64 @@
             post[k, par] = with_edges(value * slope).astype(BF16) * img_mask[...]
         return epilogue
 
+    def sum_start(i):
+        def body(d, carry):
+            other, ids = device(d)
+            pltpu.make_async_remote_copy(
+                src_ref=part.at[i, pl.ds(other * CHUNK, CHUNK)], dst_ref=got.at[i, d - 1],
+                send_sem=sum_send.at[i], recv_sem=sum_recv.at[i],
+                device_id=ids, device_id_type=pl.DeviceIdType.MESH).start()
+            return carry
+        lax.fori_loop(1, n_dev, body, 0)
+
+    def wait_all(i, sem):
+        pltpu.make_async_copy(got.at[i], got.at[i], sem.at[i]).wait()
+
+    def sum_finish(i):
+        wait_all(i, sum_recv)
+        mine = pl.ds(me * CHUNK, CHUNK)
+        total = part[i, mine]
+        for d in range(n_dev - 1):
+            total = total + got[i, d]
+        final[i, mine] = total
+
+    def spread_start(i):
+        mine = pl.ds(me * CHUNK, CHUNK)
+
+        def body(d, carry):
+            pltpu.make_async_remote_copy(
+                src_ref=final.at[i, mine], dst_ref=final.at[i, mine],
+                send_sem=all_send.at[i], recv_sem=all_recv.at[i],
+                device_id=device(d)[1], device_id_type=pl.DeviceIdType.MESH).start()
+            return carry
+        lax.fori_loop(1, n_dev, body, 0)
+
+    grads_out = (dw_first, dw_second, dw_third)
+
+    def spread_finish(i):
+        wait_all(i, all_recv)
+        return pltpu.make_async_copy(final.at[i], grads_out[i], in_sems.at[2 + i])
+
+    to_strips(0, d_one, xp, 1)
     conv_stage(xp, 1, wp.at[0], 0, PAIRS, 17, forward_epilogue(a_one, one))
     mask_rows(one)
     conv_stage(one, 0, wp.at[1], 1, PAIRS - 2, 11, forward_epilogue(a_two, two))
     mask_rows(two)
+    to_strips(1, d_two, gp, 0)
+    d_two[0, 1] = zero_row
+    d_two[PAIRS - 1, 0] = zero_row
     conv_stage(gp, 0, wp.at[3], 1, PAIRS - 2, 11, backward_epilogue(a_two, d_two))
     mask_rows(d_two)
-    wgrad_stage(two, 0, gp, own_mask, acc, dw_third, 16)
-    conv_stage(d_two, 0, wp.at[4], 1, PAIRS - 2, 11, backward_epilogue(a_one, d_one))
+    wgrad_stage(two, 0, gp, own_mask, acc, part.at[2], 16)
+    conv_stage(d_two, 0, wp.at[4], 1, 22, 11, backward_epilogue(a_one, d_one))
+    sum_start(2)
+    conv_stage(d_two, 0, wp.at[4], 23, 44, 11, backward_epilogue(a_one, d_one))
     mask_rows(d_one)
-    wgrad_stage(one, 0, d_two, own_mask, acc, dw_second, 16)
-    wgrad_stage(xp, 1, d_one, own_mask, acc, dw_first, 16)
+    wgrad_stage(one, 0, d_two, own_mask, acc, part.at[1], 16)
+    sum_finish(2)
+    wgrad_stage(xp, 1, d_one, own_mask, acc, part.at[0], 16)
+    spread_start(2)
+    sum_start(1)
 
     per_out = 4
     out_steps = OWN_PAIRS // per_out
@@ -208,7 +315,7 @@
     def store(dst, s, slot):
         return pltpu.make_async_copy(outs.at[slot], dst.at[pl.ds(s * 2 * per_out, 2 * per_out)], out_sems.at[slot])
 
-    def final_stage(src, wp_ref, skip, skip_off, dst):
+    def final_stage(src, wp_ref, skip, skip_off, dst, hooks):
         def body(s, carry):
             slot = lax.rem(s, 2)
 
@@ -232,66 +339,93 @@
                     outs[slot, line] = wide[line, 8 + COL_HALO:8 + COL_HALO + TILE].astype(BF16)
             store(dst, s, slot).start()
             return carry
-        lax.fori_loop(0, out_steps, body, 0)
+        start = 0
+        for stop, hook in list(hooks) + [(out_steps, None)]:
+            lax.fori_loop(start, stop, body, 0)
+            if hook is not None:
+                hook()
+            start = stop
         for s in range(out_steps - 2, out_steps):
             store(dst, s, s % 2).wait()
 
-    final_stage(two, wp.at[2], xp, 1, block_out)
-    final_stage(d_one, wp.at[5], gp, 0, grad_image)
-
-
-def border_pad(tile, n_rows, n_cols):
-    down_pairs = [(source, source + 1) for source in range(n_rows - 1)]
-    up_pairs = [(source + 1, source) for source in range(n_rows - 1)]
-    from_above = lax.ppermute(tile[tile.shape[0] - ROW_HALO:], 'row', down_pairs)
-    from_below = lax.ppermute(tile[:ROW_HALO], 'row', up_pairs)
-    taller = jnp.concatenate([from_above, tile, from_below], axis=0)
-    right_pairs = [(source, source + 1) for source in range(n_cols - 1)]
-    left_pairs = [(source + 1, source) for source in range(n_cols - 1)]
-    from_left = lax.ppermute(taller[:, taller.shape[1] - COL_HALO:], 'col', right_pairs)
-    from_right = lax.ppermute(taller[:, :COL_HALO], 'col', left_pairs)
-    return jnp.concatenate([from_left, taller, from_right], axis=1)
+    def mid_one():
+        sum_start(0)
+
+    def mid_two():
+        sum_finish(1)
+
+    final_stage(two, wp.at[2], xp, 1, block_out, [(1, mid_one), (15, mid_two)])
+    spread_start(1)
+    sum_finish(0)
+    copy_three = spread_finish(2)
+    copy_three.start()
+    final_stage(d_one, wp.at[5], gp, 0, grad_image, [(1, lambda: spread_start(0))])
+    copy_two = spread_finish(1)
+    copy_two.start()
+    copy_one = spread_finish(0)
+    copy_one.start()
+    for i in range(3):
+        wait_all(i, sum_send)
+        wait_all(i, all_send)
+    for i in range(2):
+        for n, (dr, dc) in enumerate(directions()):
+            @pl.when(exists(dr, dc))
+            def _():
+                halo_copy(i, n, dr, dc).wait_send()
+    copy_three.wait()
+    copy_two.wait()
+    copy_one.wait()
 
 
 def solution(mesh):
-    n_rows = mesh.shape['row']
-    n_cols = mesh.shape['col']
+    assert (mesh.shape['row'], mesh.shape['col']) == (N_ROWS, N_COLS)
     act_spec = P(None, 'row', 'col', None)
     padded = (PAIRS, 2, PAD_STEPS, STRIPS, CH)
     plain = (PAIRS, 2, STEPS, STRIPS, CH)
     tile_shape = jax.ShapeDtypeStruct((TILE, TILE, CH), BF16)
-    dw_shape = jax.ShapeDtypeStruct((3, 3, CH, CH), F32)
+    dw_shape = jax.ShapeDtypeStruct((9 * CH, CH), F32)
     hbm = pl.BlockSpec(memory_space=pl.ANY)
     vmem = pl.BlockSpec(memory_space=pltpu.VMEM)
+    n_dev = N_ROWS * N_COLS
     call = pl.pallas_call(
         block_kernel,
         out_shape=(tile_shape, tile_shape, dw_shape, dw_shape, dw_shape),
-        in_specs=[hbm, hbm, vmem, vmem, vmem],
-        out_specs=(hbm, hbm, vmem, vmem, vmem),
+        in_specs=[hbm] * 6 + [vmem] * 3,
+        out_specs=(hbm,) * 5,
         scratch_shapes=[
             pltpu.VMEM((PAIRS + 2, 2, PAD_STEPS, STRIPS, CH), BF16),
             pltpu.VMEM(padded, BF16), pltpu.VMEM(padded, BF16), pltpu.VMEM(padded, BF16),
             pltpu.VMEM(padded, BF16), pltpu.VMEM(padded, BF16),
             pltpu.VMEM(plain, BF16), pltpu.VMEM(plain, BF16),
             pltpu.VMEM((6, 12 * CH, 2 * CH), BF16),
-            pltpu.VMEM((2, STAGE_ROWS, EXT_COLS, CH), BF16),
+            pltpu.VMEM((2, 2, EXT_ROWS, QUAD, CH), BF16),
             pltpu.VMEM((STAGE_ROWS, EXT_COLS + 16, CH), F32),
             pltpu.VMEM((2, 8, TILE, CH), BF16),
             pltpu.VMEM((3 * CH, 3 * CH), F32),
             pltpu.VMEM((PAD_STEPS, STRIPS, CH), BF16),
             pltpu.VMEM((PAD_STEPS, STRIPS, CH), BF16),
+            pltpu.VMEM((3, 9 * CH, CH), F32),
+            pltpu.VMEM((3, n_dev - 1, CHUNK, CH), F32),
+            pltpu.VMEM((3, 9 * CH, CH), F32),
+            pltpu.SemaphoreType.DMA((5,)),
             pltpu.SemaphoreType.DMA((2,)),
-            pltpu.SemaphoreType.DMA((2,)),
+            pltpu.SemaphoreType.DMA((2, 8)),
+            pltpu.SemaphoreType.DMA((2, 8)),
+            pltpu.SemaphoreType.DMA((3,)),
+            pltpu.SemaphoreType.DMA((3,)),
+            pltpu.SemaphoreType.DMA((3,)),
+            pltpu.SemaphoreType.DMA((3,)),
         ],
-        compiler_params=pltpu.CompilerParams(vmem_limit_bytes=67043328),
+        compiler_params=pltpu.CompilerParams(vmem_limit_bytes=67043328, collective_id=0, has_side_effects=True),
         name='block',
     )
 
     def local_block(image, w_first, w_second, w_third, grad_out):
-        image_ext = border_pad(image[0], n_rows, n_cols)
-        grad_ext = border_pad(grad_out[0], n_rows, n_cols)
-        out, dx, dw1, dw2, dw3 = call(image_ext, grad_ext, w_first, w_second, w_third)
-        dw1, dw2, dw3 = lax.psum((dw1, dw2, dw3), ('row', 'col'))
-        return out[None], dx[None], dw1, dw2, dw3
+        views = []
+        for tile in (image, grad_out):
+            views += [tile.reshape(TILE, TILE, CH), tile.reshape(TILE, TILE // QUAD, QUAD, CH), tile.reshape(OWN_PAIRS, 2, TILE // STRIPS, STRIPS, CH)]
+        out, dx, dw1, dw2, dw3 = call(*views, w_first, w_second, w_third)
+        shape = (3, 3, CH, CH)
+        return out[None], dx[None], dw1.reshape(shape), dw2.reshape(shape), dw3.reshape(shape)
 
     return jax.shard_map(local_block, mesh=mesh, in_specs=(act_spec, P(), P(), P(), act_spec), out_specs=(act_spec, act_spec, P(), P(), P()), check_vma=False)

time: 248 us -> 127 us (0.51)
  waiting for transfers between devices: 83.4 us -> 0 us
  starting transfers between devices: 21 us -> 0 us
  between operations: 14.2 us -> 0.66 us
  other arithmetic: 12.3 us -> 0 us
  Pallas kernels: 109 us -> 117 us
  local copies, waits for them, and re-layouts: 6.91 us -> 9.42 us
    psum x1 -> x0, waiting for transfers between devices: 71.2 us -> none  [local_block(): dw1, dw2, dw3 = lax.psum((dw1, dw2, dw3), ('row', 'col'))]
    ppermute x8 -> x0, starting transfers between devices: 21 us -> none  [the longest x2 7.96 us: border_pad(): lax.ppermute(tile[tile.shape[0] - ROW_HALO:], 'row', down_pairs)]
    ppermute x8 -> x0, waiting for transfers between devices: 12.2 us -> none  [the longest x2 6.2 us: border_pad(): from_right = lax.ppermute(taller[:, :COL_HALO], 'col', left_pairs)]
    concatenate x2 -> x0, other arithmetic: 11 us -> none  [border_pad(): return jnp.concatenate([from_left, taller, from_right], axis=1)]
    pallas_call x1, Pallas kernels: 109 us -> 117 us  [local_block(): out, dx, dw1, dw2, dw3 = call(*views, w_first, w_second, w_third)]
    unnamed x7 -> x13, local copies, waits for them, and re-layouts: 5.76 us -> 9.42 us
  transfers between devices with their start and end apart: 9 -> 0, of which waited for: 4 -> 0; matrix products, arithmetic and copies ran while one was open for 2% -> 0% of each run, Pallas kernels for 0% -> 0%
where the time goes in v2:
time: 127 us
  Pallas kernels  117 us (92%)
  local copies, waits for them, and re-layouts  9.42 us (7%)
    pallas_call x1, Pallas kernels, local_block(): out, dx, dw1, dw2, dw3 = call(*views, w_first, w_second, w_third)  117 us
    unnamed x13, local copies, waits for them, and re-layouts  9.42 us

profile of v2, /device:TPU:0, one launch (start us, length us, event | category | flops | bytes accessed | tf_op | source)
XLA Modules:
  0.0 127.0 jit_solution(16143130019337992927)
XLA Ops:
  0.6 117.0 %block.1 = (bf16[128,128,128]{2,1,0:T(8,128)(2,1)}, bf16[128,128,128]{2,1,0:T(8,128)(2,1)}, f32[1152,128]{1,0:T(8,128)}, f32[1152,128]{1,0:T(8,128)}, f32[1152,128]{1,0:T(8,128)}) custom-call(bf16[128,128,128]{2,1,0:T(8,128)(2,1)} %bitcast.11, bf16[128,32,4,128]{3,2,1,0:T(4,128)(2,1)} %bitcast.12, bf16[64,2,8,16,128]{4,3,2,1,0:T(8,128)(2,1)} %bitcast.13, ...), custom_call_target="tpu_custom_call" | custom-call | tf_op jit(solution)/shard_map/block/pallas_call | solution.py:427
  117.6 0.0 copy-start
  117.6 4.9 %copy.15 = bf16[1,128,128,128]{3,2,1,0:T(8,128)(2,1)} copy(bf16[1,128,128,128]{3,2,1,0:T(8,128)(2,1)} %bitcast.18) | data formatting | bytes 8388608
  122.6 0.0 copy-done
  122.6 0.0 copy-start.3
  122.6 0.0 copy-start.2
  122.6 0.0 copy-start.1
  122.6 2.0 %copy.16 = bf16[1,128,128,128]{3,2,1,0:T(8,128)(2,1)} copy(bf16[1,128,128,128]{3,2,1,0:T(8,128)(2,1)S(1)} %bitcast.17) | data formatting | bytes 8388608
  124.6 0.0 copy-done.3
  124.6 0.8 copy.17
  125.4 0.0 copy-done.2
  125.4 0.8 copy.18
  126.2 0.0 copy-done.1
  126.2 0.8 copy.19
Async XLA Ops:
  117.6 5.0 %copy-start = (bf16[128,128,128]{2,1,0:T(8,128)(2,1)S(1)}, bf16[128,128,128]{2,1,0:T(8,128)(2,1)}, u32[]{:S(2)}) copy-start(bf16[128,128,128]{2,1,0:T(8,128)(2,1)} %get-tuple-element.11) | copy-start | bytes 12582916
  122.6 2.0 %copy-start.3 = (f32[1152,128]{1,0:T(8,128)S(1)}, f32[1152,128]{1,0:T(8,128)}, u32[]{:S(2)}) copy-start(f32[1152,128]{1,0:T(8,128)} %get-tuple-element.12) | copy-start | bytes 1769476
  122.6 2.8 %copy-start.2 = (f32[1152,128]{1,0:T(8,128)S(1)}, f32[1152,128]{1,0:T(8,128)}, u32[]{:S(2)}) copy-start(f32[1152,128]{1,0:T(8,128)} %get-tuple-element.13) | copy-start | bytes 1769476
  122.6 3.7 %copy-start.1 = (f32[1152,128]{1,0:T(8,128)S(1)}, f32[1152,128]{1,0:T(8,128)}, u32[]{:S(2)}) copy-start(f32[1152,128]{1,0:T(8,128)} %get-tuple-element.14) | copy-start | bytes 1769476

commit v3 on v2

--- a/solution.py
+++ b/solution.py
@@ -24,10 +24,12 @@
 OWN_PAIRS = TILE // 2
 EXT_ROWS = TILE + 2 * ROW_HALO
 EXT_COLS = TILE + 2 * COL_HALO
-STAGE_ROWS = 8
 QUAD = 4
 N_ROWS = 4
 N_COLS = 4
+SIDES = 4
+SIDE_ROWS = TILE // SIDES
+HALF = 9 * CH // 2
 CHUNK = 9 * CH // (N_ROWS * N_COLS)
 
 
@@ -59,7 +61,14 @@
         wp_ref[pl.ds((q * 4) * CH, CH), pl.ds(CH, CH)] = zero
 
 
-def conv_stage(src, off, wp, first, count, per_step, epilogue):
+def run_hooks(hooks, step):
+    for at, hook in hooks:
+        @pl.when(step == at)
+        def _():
+            hook()
+
+
+def conv_stage(src, off, wp, first, count, per_step, epilogue, hooks=()):
     def body(step, carry):
         base = first + step * per_step
         for j in range(per_step):
@@ -72,6 +81,7 @@
             acc = jnp.dot(jnp.concatenate(parts, axis=1), wp[...], preferred_element_type=F32)
             for par in range(2):
                 epilogue(k, par, j, acc[:, par * CH:(par + 1) * CH].reshape(STEPS, STRIPS, CH))
+        run_hooks(hooks, step)
         return carry
     lax.fori_loop(0, count // per_step, body, 0)
 
@@ -82,7 +92,7 @@
     return jnp.concatenate([left, value, right], axis=0)
 
 
-def wgrad_stage(val, off, grad, own_mask, acc, out, per_step):
+def wgrad_stage(val, off, grad, own_mask, acc, out, per_step, hooks=()):
     dims = (((0,), (0,)), ((), ()))
     flat = per_step * STEPS * STRIPS
     acc[...] = jnp.zeros_like(acc)
@@ -104,6 +114,7 @@
         both = jnp.concatenate([shifted[0][2], shifted[1][2]], axis=1)
         last = lax.dot_general(jnp.concatenate(rows, axis=1), both, dims, preferred_element_type=F32)
         acc[:, 2 * CH:3 * CH] += last[0:3 * CH, 0:CH] + last[CH:4 * CH, CH:2 * CH]
+        run_hooks(hooks, step)
         return carry
 
     lax.fori_loop(0, OWN_PAIRS // per_step, body, 0)
@@ -119,8 +130,8 @@
 def block_kernel(image, image_quads, image_pairs, grad, grad_quads, grad_pairs, w_first, w_second, w_third,
                  block_out, grad_image, dw_first, dw_second, dw_third,
                  xp, one, two, gp, d_two, d_one, a_one, a_two, wp,
-                 halo, wide, outs, acc, img_mask, own_mask, part, got, final,
-                 in_sems, out_sems, halo_send, halo_recv, sum_send, sum_recv, all_send, all_recv):
+                 halo, wide, outs, acc, img_mask, own_mask, part, pair_got, half, got, final,
+                 in_sems, out_sems, halo_send, halo_recv, sum_send, sum_recv):
     n_rows, n_cols = N_ROWS, N_COLS
     n_dev = n_rows * n_cols
     row_id = lax.axis_index('row')
@@ -156,8 +167,8 @@
     zero_row = jnp.zeros((PAD_STEPS, STRIPS, CH), BF16)
     xp[0, 1] = zero_row
     xp[PAIRS + 1, 0] = zero_row
-    wide[:, 0:16] = jnp.zeros((STAGE_ROWS, 16, CH), F32)
-    wide[:, TILE + 16:TILE + 32] = jnp.zeros((STAGE_ROWS, 16, CH), F32)
+    wide[:, 0:16] = jnp.zeros((16, 16, CH), F32)
+    wide[:, TILE + 16:TILE + 32] = jnp.zeros((16, 16, CH), F32)
 
     @pl.when(col_id == 0)
     def _():
@@ -171,18 +182,19 @@
 
     pl.semaphore_wait(barrier, n_dev - 1)
 
-    def halo_copy(i, n, dr, dc):
+    def halo_copy(i, n, dr, dc, chunk=0):
         quads, pairs, natural = ((image_quads, image_pairs, d_one), (grad_quads, grad_pairs, d_two))[i]
         if dc == 0:
             src = pairs.at[pl.ds(0, 2)] if dr < 0 else pairs.at[pl.ds(OWN_PAIRS - 2, 2)]
             dst = natural.at[pl.ds(PAIRS - 2, 2) if dr < 0 else pl.ds(0, 2), :, pl.ds(0, 8)]
         else:
-            rows = (pl.ds(0, ROW_HALO), pl.ds(0, TILE), pl.ds(TILE - ROW_HALO, ROW_HALO))[dr + 1]
-            into = (pl.ds(EXT_ROWS - ROW_HALO, ROW_HALO), pl.ds(ROW_HALO, TILE), pl.ds(0, ROW_HALO))[dr + 1]
+            side = pl.ds(chunk * SIDE_ROWS, SIDE_ROWS)
+            rows = (pl.ds(0, ROW_HALO), side, pl.ds(TILE - ROW_HALO, ROW_HALO))[dr + 1]
+            into = (pl.ds(EXT_ROWS - ROW_HALO, ROW_HALO), pl.ds(ROW_HALO + chunk * SIDE_ROWS, SIDE_ROWS), pl.ds(0, ROW_HALO))[dr + 1]
             src = quads.at[rows, 0 if dc < 0 else TILE // QUAD - 1]
             dst = halo.at[i, 1 if dc < 0 else 0, into]
         return pltpu.make_async_remote_copy(
-            src_ref=src, dst_ref=dst, send_sem=halo_send.at[i, n], recv_sem=halo_recv.at[i, n],
+            src_ref=src, dst_ref=dst, send_sem=halo_send.at[i, n, chunk], recv_sem=halo_recv.at[i, n, chunk],
             device_id={'col': col_id + dc, 'row': row_id + dr}, device_id_type=pl.DeviceIdType.MESH)
 
     def exists(dr, dc):
@@ -193,20 +205,35 @@
                 ok = one_ok if ok is None else ok & one_ok
         return ok
 
-    for i in range(2):
-        for n, (dr, dc) in enumerate(directions()):
-            @pl.when(exists(dr, dc))
+    around = list(enumerate(directions()))
+    sides = [(n, d) for n, d in around if d[0] == 0]
+    over = [(n, d) for n, d in around if d[0] == 1]
+    under = [(n, d) for n, d in around if d[0] == -1]
+
+    def halo_do(i, group, chunk, what):
+        for n, (dr, dc) in group:
+            flip = -1 if what == 'recv' else 1
+
+            @pl.when(exists(flip * dr, flip * dc))
             def _():
-                halo_copy(i, n, dr, dc).start()
+                copy = halo_copy(i, n, dr, dc, chunk)
+                if what == 'start':
+                    copy.start()
+                elif what == 'recv':
+                    copy.wait_recv()
+                else:
+                    copy.wait_send()
+
+    def halo_start(i):
+        halo_do(i, over, 0, 'start')
+        for chunk in range(SIDES):
+            halo_do(i, sides, chunk, 'start')
+        halo_do(i, under, 0, 'start')
+
+    halo_start(0)
 
     for i, (w_ref, back) in enumerate(((w_first, False), (w_second, False), (w_third, False), (w_third, True), (w_second, True), (w_first, True))):
         pack_weights(w_ref, wp.at[i], back)
-
-    def halo_wait(i):
-        for n, (dr, dc) in enumerate(directions()):
-            @pl.when(exists(-dr, -dc))
-            def _():
-                halo_copy(i, n, dr, dc).wait_recv()
 
     def mask_rows(ref, off=0):
         zeros = jnp.zeros((2, 2, PAD_STEPS, STRIPS, CH), BF16)
@@ -219,23 +246,19 @@
         def _():
             ref[off + PAIRS - 2:off + PAIRS] = zeros
 
-    def to_strips(i, natural, dst, off):
-        local(i).wait()
-        halo_wait(i)
-
+    def to_strips(i, natural, dst, off, first, count):
         def body(b, carry):
-            for r in range(STAGE_ROWS):
-                k, par = b * (STAGE_ROWS // 2) + r // 2, r % 2
+            for r in range(4):
+                k, par = first + 2 * b + r // 2, r % 2
                 wide[r, 16:16 + TILE] = natural[k, par, 0:8].reshape(TILE, CH).astype(F32)
                 wide[r, 16 - QUAD:16] = halo[i, 0, 2 * k + par].astype(F32)
                 wide[r, 16 + TILE:16 + TILE + QUAD] = halo[i, 1, 2 * k + par].astype(F32)
-            for r in range(STAGE_ROWS):
-                k, par = b * (STAGE_ROWS // 2) + r // 2, r % 2
+            for r in range(4):
+                k, par = first + 2 * b + r // 2, r % 2
                 tiles = [wide[r, pl.ds(7 + t, STRIPS, stride=STEPS)] for t in range(PAD_STEPS)]
                 dst[off + k, par] = jnp.stack(tiles).astype(BF16)
             return carry
-        lax.fori_loop(0, EXT_ROWS // STAGE_ROWS, body, 0)
-        mask_rows(dst, off)
+        lax.fori_loop(0, count // 2, body, 0)
 
     def forward_epilogue(pre, post):
         def epilogue(k, par, j, value):
@@ -250,66 +273,117 @@
             post[k, par] = with_edges(value * slope).astype(BF16) * img_mask[...]
         return epilogue
 
-    def sum_start(i):
+    core = lax.rem(row_id, 2)
+    chip = col_id * 2 + row_id // 2
+    n_chips = n_dev // 2
+    partner = {'col': col_id, 'row': row_id + 1 - 2 * core}
+    my_half = pl.ds(core * HALF, HALF)
+    mine = pl.ds(core * HALF + chip * CHUNK, CHUNK)
+    MESH = pl.DeviceIdType.MESH
+    grads_out = (dw_first, dw_second, dw_third)
+
+    def pair_copy(i):
+        return pltpu.make_async_remote_copy(
+            src_ref=part.at[i, pl.ds((1 - core) * HALF, HALF)], dst_ref=pair_got.at[i],
+            send_sem=sum_send.at[i, 0], recv_sem=sum_recv.at[i, 0], device_id=partner, device_id_type=MESH)
+
+    def pair_start(i):
+        pair_copy(i).start()
+
+    def pair_add(i):
+        pair_copy(i).wait_recv()
+        half[i] = part[i, my_half] + pair_got[i]
+
+    def to_chips(make):
         def body(d, carry):
-            other, ids = device(d)
-            pltpu.make_async_remote_copy(
-                src_ref=part.at[i, pl.ds(other * CHUNK, CHUNK)], dst_ref=got.at[i, d - 1],
-                send_sem=sum_send.at[i], recv_sem=sum_recv.at[i],
-                device_id=ids, device_id_type=pl.DeviceIdType.MESH).start()
+            other = lax.rem(chip + d, n_chips)
+            make(d, other, {'col': other // 2, 'row': lax.rem(other, 2) * 2 + core}).start()
             return carry
-        lax.fori_loop(1, n_dev, body, 0)
-
-    def wait_all(i, sem):
-        pltpu.make_async_copy(got.at[i], got.at[i], sem.at[i]).wait()
-
-    def sum_finish(i):
-        wait_all(i, sum_recv)
-        mine = pl.ds(me * CHUNK, CHUNK)
-        total = part[i, mine]
-        for d in range(n_dev - 1):
+        lax.fori_loop(1, n_chips, body, 0)
+
+    def chunk_start(i):
+        to_chips(lambda d, other, ids: pltpu.make_async_remote_copy(
+            src_ref=half.at[i, pl.ds(other * CHUNK, CHUNK)], dst_ref=got.at[i, d - 1],
+            send_sem=sum_send.at[i, 1], recv_sem=sum_recv.at[i, 1], device_id=ids, device_id_type=MESH))
+
+    def wait_bytes(i, sem):
+        pltpu.make_async_copy(got.at[i], got.at[i], sem).wait()
+
+    def chunk_add(i):
+        wait_bytes(i, sum_recv.at[i, 1])
+        total = half[i, pl.ds(chip * CHUNK, CHUNK)]
+        for d in range(n_chips - 1):
             total = total + got[i, d]
         final[i, mine] = total
 
     def spread_start(i):
-        mine = pl.ds(me * CHUNK, CHUNK)
-
-        def body(d, carry):
-            pltpu.make_async_remote_copy(
-                src_ref=final.at[i, mine], dst_ref=final.at[i, mine],
-                send_sem=all_send.at[i], recv_sem=all_recv.at[i],
-                device_id=device(d)[1], device_id_type=pl.DeviceIdType.MESH).start()
-            return carry
-        lax.fori_loop(1, n_dev, body, 0)
-
-    grads_out = (dw_first, dw_second, dw_third)
-
-    def spread_finish(i):
-        wait_all(i, all_recv)
+        to_chips(lambda d, other, ids: pltpu.make_async_remote_copy(
+            src_ref=final.at[i, mine], dst_ref=final.at[i, mine],
+            send_sem=sum_send.at[i, 2], recv_sem=sum_recv.at[i, 2], device_id=ids, device_id_type=MESH))
+
+    def return_copy(i):
+        return pltpu.make_async_remote_copy(
+            src_ref=final.at[i, my_half], dst_ref=final.at[i, my_half],
+            send_sem=sum_send.at[i, 3], recv_sem=sum_recv.at[i, 3], device_id=partner, device_id_type=MESH)
+
+    def return_start(i):
+        wait_bytes(i, sum_recv.at[i, 2])
+        return_copy(i).start()
+
+    def out_copy(i):
         return pltpu.make_async_copy(final.at[i], grads_out[i], in_sems.at[2 + i])
 
-    to_strips(0, d_one, xp, 1)
-    conv_stage(xp, 1, wp.at[0], 0, PAIRS, 17, forward_epilogue(a_one, one))
+    def out_start(i):
+        return_copy(i).wait_recv()
+        out_copy(i).start()
+
+    local(0).wait()
+    halo_do(0, over, 0, 'recv')
+    to_strips(0, d_one, xp, 1, 0, 2)
+    first_step = forward_epilogue(a_one, one)
+
+    def first_body(c, carry):
+        halo_do(0, sides, c, 'recv')
+        to_strips(0, d_one, xp, 1, 2 + c * 16, 16)
+
+        @pl.when((c == 0) & (row_id == 0))
+        def _():
+            xp[1:3] = jnp.zeros((2, 2, PAD_STEPS, STRIPS, CH), BF16)
+        conv_stage(xp, 1, wp.at[0], c * 16, 16, 16, first_step)
+        return carry
+    lax.fori_loop(0, SIDES, first_body, 0)
+    halo_do(0, under, 0, 'recv')
+    halo_start(1)
+    to_strips(0, d_one, xp, 1, PAIRS - 2, 2)
+    mask_rows(xp, 1)
+    conv_stage(xp, 1, wp.at[0], 64, 4, 4, first_step)
     mask_rows(one)
     conv_stage(one, 0, wp.at[1], 1, PAIRS - 2, 11, forward_epilogue(a_two, two))
     mask_rows(two)
-    to_strips(1, d_two, gp, 0)
+    local(1).wait()
+    halo_do(1, over, 0, 'recv')
+    for chunk in range(SIDES):
+        halo_do(1, sides, chunk, 'recv')
+    halo_do(1, under, 0, 'recv')
+    to_strips(1, d_two, gp, 0, 0, PAIRS)
+    mask_rows(gp)
     d_two[0, 1] = zero_row
     d_two[PAIRS - 1, 0] = zero_row
     conv_stage(gp, 0, wp.at[3], 1, PAIRS - 2, 11, backward_epilogue(a_two, d_two))
     mask_rows(d_two)
+
+    def call(fn, i):
+        return lambda: fn(i)
+
     wgrad_stage(two, 0, gp, own_mask, acc, part.at[2], 16)
-    conv_stage(d_two, 0, wp.at[4], 1, 22, 11, backward_epilogue(a_one, d_one))
-    sum_start(2)
-    conv_stage(d_two, 0, wp.at[4], 23, 44, 11, backward_epilogue(a_one, d_one))
+    conv_stage(d_two, 0, wp.at[4], 1, PAIRS - 2, 11, backward_epilogue(a_one, d_one),
+               [(0, call(pair_start, 2)), (2, call(pair_add, 2)), (3, call(chunk_start, 2))])
     mask_rows(d_one)
-    wgrad_stage(one, 0, d_two, own_mask, acc, part.at[1], 16)
-    sum_finish(2)
-    wgrad_stage(xp, 1, d_one, own_mask, acc, part.at[0], 16)
-    spread_start(2)
-    sum_start(1)
-
-    per_out = 4
+    wgrad_stage(one, 0, d_two, own_mask, acc, part.at[1], 16, [(2, call(chunk_add, 2)), (3, call(spread_start, 2))])
+    wgrad_stage(xp, 1, d_one, own_mask, acc, part.at[0], 16,
+                [(0, call(pair_start, 1)), (1, call(pair_add, 1)), (2, call(chunk_start, 1)), (3, call(return_start, 2))])
+
+    per_out = 8
     out_steps = OWN_PAIRS // per_out
 
     def store(dst, s, slot):
@@ -338,43 +412,30 @@
                         wide[line, pl.ds(8 + t, STRIPS, stride=STEPS)] = value[t]
                     outs[slot, line] = wide[line, 8 + COL_HALO:8 + COL_HALO + TILE].astype(BF16)
             store(dst, s, slot).start()
+            run_hooks(hooks, s)
             return carry
-        start = 0
-        for stop, hook in list(hooks) + [(out_steps, None)]:
-            lax.fori_loop(start, stop, body, 0)
-            if hook is not None:
-                hook()
-            start = stop
+        lax.fori_loop(0, out_steps, body, 0)
         for s in range(out_steps - 2, out_steps):
             store(dst, s, s % 2).wait()
 
-    def mid_one():
-        sum_start(0)
-
-    def mid_two():
-        sum_finish(1)
-
-    final_stage(two, wp.at[2], xp, 1, block_out, [(1, mid_one), (15, mid_two)])
-    spread_start(1)
-    sum_finish(0)
-    copy_three = spread_finish(2)
-    copy_three.start()
-    final_stage(d_one, wp.at[5], gp, 0, grad_image, [(1, lambda: spread_start(0))])
-    copy_two = spread_finish(1)
-    copy_two.start()
-    copy_one = spread_finish(0)
-    copy_one.start()
+    final_stage(two, wp.at[2], xp, 1, block_out,
+                [(0, call(pair_start, 0)), (1, call(pair_add, 0)), (2, call(chunk_start, 0)), (3, call(chunk_add, 1)),
+                 (4, call(spread_start, 1)), (5, call(out_start, 2)), (7, call(chunk_add, 0))])
+    final_stage(d_one, wp.at[5], gp, 0, grad_image,
+                [(0, call(spread_start, 0)), (3, call(return_start, 1)), (5, call(out_start, 1)), (6, call(return_start, 0))])
+    out_start(0)
     for i in range(3):
-        wait_all(i, sum_send)
-        wait_all(i, all_send)
+        pair_copy(i).wait_send()
+        wait_bytes(i, sum_send.at[i, 1])
+        wait_bytes(i, sum_send.at[i, 2])
+        return_copy(i).wait_send()
     for i in range(2):
-        for n, (dr, dc) in enumerate(directions()):
-            @pl.when(exists(dr, dc))
-            def _():
-                halo_copy(i, n, dr, dc).wait_send()
-    copy_three.wait()
-    copy_two.wait()
-    copy_one.wait()
+        halo_do(i, over, 0, 'send')
+        for chunk in range(SIDES):
+            halo_do(i, sides, chunk, 'send')
+        halo_do(i, under, 0, 'send')
+    for i in range(3):
+        out_copy(i).wait()
 
 
 def solution(mesh):
@@ -399,22 +460,22 @@
             pltpu.VMEM(plain, BF16), pltpu.VMEM(plain, BF16),
             pltpu.VMEM((6, 12 * CH, 2 * CH), BF16),
             pltpu.VMEM((2, 2, EXT_ROWS, QUAD, CH), BF16),
-            pltpu.VMEM((STAGE_ROWS, EXT_COLS + 16, CH), F32),
-            pltpu.VMEM((2, 8, TILE, CH), BF16),
+            pltpu.VMEM((16, EXT_COLS + 16, CH), F32),
+            pltpu.VMEM((2, 16, TILE, CH), BF16),
             pltpu.VMEM((3 * CH, 3 * CH), F32),
             pltpu.VMEM((PAD_STEPS, STRIPS, CH), BF16),
             pltpu.VMEM((PAD_STEPS, STRIPS, CH), BF16),
             pltpu.VMEM((3, 9 * CH, CH), F32),
-            pltpu.VMEM((3, n_dev - 1, CHUNK, CH), F32),
+            pltpu.VMEM((3, HALF, CH), F32),
+            pltpu.VMEM((3, HALF, CH), F32),
+            pltpu.VMEM((3, n_dev // 2 - 1, CHUNK, CH), F32),
             pltpu.VMEM((3, 9 * CH, CH), F32),
             pltpu.SemaphoreType.DMA((5,)),
             pltpu.SemaphoreType.DMA((2,)),
-            pltpu.SemaphoreType.DMA((2, 8)),
-            pltpu.SemaphoreType.DMA((2, 8)),
-            pltpu.SemaphoreType.DMA((3,)),
-            pltpu.SemaphoreType.DMA((3,)),
-            pltpu.SemaphoreType.DMA((3,)),
-            pltpu.SemaphoreType.DMA((3,)),
+            pltpu.SemaphoreType.DMA((2, 8, SIDES)),
+            pltpu.SemaphoreType.DMA((2, 8, SIDES)),
+            pltpu.SemaphoreType.DMA((3, 4)),
+            pltpu.SemaphoreType.DMA((3, 4)),
         ],
         compiler_params=pltpu.CompilerParams(vmem_limit_bytes=67043328, collective_id=0, has_side_effects=True),
         name='block',

time: 127 us -> 110 us (0.87)
  Pallas kernels: 117 us -> 100 us
    pallas_call x1, Pallas kernels: 117 us -> 100 us  [local_block(): out, dx, dw1, dw2, dw3 = call(*views, w_first, w_second, w_third)]
where the time goes in v3:
time: 110 us
  Pallas kernels  100 us (91%)
  local copies, waits for them, and re-layouts  9.42 us (9%)
    pallas_call x1, Pallas kernels, local_block(): out, dx, dw1, dw2, dw3 = call(*views, w_first, w_second, w_third)  100 us
    unnamed x13, local copies, waits for them, and re-layouts  9.42 us

profile of v3, /device:TPU:0, one launch (start us, length us, event | category | flops | bytes accessed | tf_op | source)
XLA Modules:
  0.0 110.2 jit_solution(4601658462813922772)
XLA Ops:
  0.6 100.2 %block.1 = (bf16[128,128,128]{2,1,0:T(8,128)(2,1)}, bf16[128,128,128]{2,1,0:T(8,128)(2,1)}, f32[1152,128]{1,0:T(8,128)}, f32[1152,128]{1,0:T(8,128)}, f32[1152,128]{1,0:T(8,128)}) custom-call(bf16[128,128,128]{2,1,0:T(8,128)(2,1)} %bitcast.11, bf16[128,32,4,128]{3,2,1,0:T(4,128)(2,1)} %bitcast.12, bf16[64,2,8,16,128]{4,3,2,1,0:T(8,128)(2,1)} %bitcast.13, ...), custom_call_target="tpu_custom_call" | custom-call | tf_op jit(solution)/shard_map/block/pallas_call | solution.py:488
  100.8 0.0 copy-start
  100.8 4.9 %copy.15 = bf16[1,128,128,128]{3,2,1,0:T(8,128)(2,1)} copy(bf16[1,128,128,128]{3,2,1,0:T(8,128)(2,1)} %bitcast.18) | data formatting | bytes 8388608
  105.8 0.0 copy-done
  105.8 0.0 copy-start.3
  105.8 0.0 copy-start.2
  105.8 0.0 copy-start.1
  105.8 2.0 %copy.16 = bf16[1,128,128,128]{3,2,1,0:T(8,128)(2,1)} copy(bf16[1,128,128,128]{3,2,1,0:T(8,128)(2,1)S(1)} %bitcast.17) | data formatting | bytes 8388608
  107.8 0.0 copy-done.3
  107.8 0.8 copy.17
  108.6 0.0 copy-done.2
  108.6 0.8 copy.18
  109.4 0.0 copy-done.1
  109.4 0.8 copy.19
Async XLA Ops:
  100.8 5.0 %copy-start = (bf16[128,128,128]{2,1,0:T(8,128)(2,1)S(1)}, bf16[128,128,128]{2,1,0:T(8,128)(2,1)}, u32[]{:S(2)}) copy-start(bf16[128,128,128]{2,1,0:T(8,128)(2,1)} %get-tuple-element.11) | copy-start | bytes 12582916
  105.8 2.0 %copy-start.3 = (f32[1152,128]{1,0:T(8,128)S(1)}, f32[1152,128]{1,0:T(8,128)}, u32[]{:S(2)}) copy-start(f32[1152,128]{1,0:T(8,128)} %get-tuple-element.12) | copy-start | bytes 1769476
  105.8 2.8 %copy-start.2 = (f32[1152,128]{1,0:T(8,128)S(1)}, f32[1152,128]{1,0:T(8,128)}, u32[]{:S(2)}) copy-start(f32[1152,128]{1,0:T(8,128)} %get-tuple-element.13) | copy-start | bytes 1769476
  105.8 3.7 %copy-start.1 = (f32[1152,128]{1,0:T(8,128)S(1)}, f32[1152,128]{1,0:T(8,128)}, u32[]{:S(2)}) copy-start(f32[1152,128]{1,0:T(8,128)} %get-tuple-element.14) | copy-start | bytes 1769476

commit v4 on v3

--- a/solution.py
+++ b/solution.py
@@ -27,19 +27,26 @@
 QUAD = 4
 N_ROWS = 4
 N_COLS = 4
+PIECES = 4
+COPY_PARTS = (8, 8, 1, 1, 1)
 SIDES = 4
 SIDE_ROWS = TILE // SIDES
 HALF = 9 * CH // 2
 CHUNK = 9 * CH // (N_ROWS * N_COLS)
 
 
+def gelu_arg(value, square):
+    return jnp.tanh(value * (GELU_SCALE + (GELU_SCALE * GELU_CUBIC) * square))
+
+
 def gelu_tanh(value):
-    return 0.5 * value * (1.0 + jnp.tanh(GELU_SCALE * (value + GELU_CUBIC * value * value * value)))
+    return 0.5 * value * (1.0 + gelu_arg(value, value * value))
 
 
 def gelu_slope(value):
-    tanh_val = jnp.tanh(GELU_SCALE * (value + GELU_CUBIC * value * value * value))
-    return 0.5 * (1.0 + tanh_val) + 0.5 * value * (1.0 - tanh_val * tanh_val) * GELU_SCALE * (1.0 + 3.0 * GELU_CUBIC * value * value)
+    square = value * value
+    s = 0.5 + 0.5 * gelu_arg(value, square)
+    return s + (s * (1.0 - s) * value) * (2.0 * GELU_SCALE + (6.0 * GELU_SCALE * GELU_CUBIC) * square)
 
 
 def row_at(ref, k, r, off):
@@ -282,16 +289,20 @@
     MESH = pl.DeviceIdType.MESH
     grads_out = (dw_first, dw_second, dw_third)
 
-    def pair_copy(i):
-        return pltpu.make_async_remote_copy(
-            src_ref=part.at[i, pl.ds((1 - core) * HALF, HALF)], dst_ref=pair_got.at[i],
-            send_sem=sum_send.at[i, 0], recv_sem=sum_recv.at[i, 0], device_id=partner, device_id_type=MESH)
+    def pieces(make):
+        for n in range(PIECES):
+            make(n * (HALF // PIECES), HALF // PIECES).start()
+
+    def wait_half(i, sem):
+        pltpu.make_async_copy(half.at[i], half.at[i], sem).wait()
 
     def pair_start(i):
-        pair_copy(i).start()
+        pieces(lambda at, size: pltpu.make_async_remote_copy(
+            src_ref=part.at[i, pl.ds((1 - core) * HALF + at, size)], dst_ref=pair_got.at[i, pl.ds(at, size)],
+            send_sem=sum_send.at[i, 0], recv_sem=sum_recv.at[i, 0], device_id=partner, device_id_type=MESH))
 
     def pair_add(i):
-        pair_copy(i).wait_recv()
+        wait_half(i, sum_recv.at[i, 0])
         half[i] = part[i, my_half] + pair_got[i]
 
     def to_chips(make):
@@ -321,20 +332,17 @@
             src_ref=final.at[i, mine], dst_ref=final.at[i, mine],
             send_sem=sum_send.at[i, 2], recv_sem=sum_recv.at[i, 2], device_id=ids, device_id_type=MESH))
 
-    def return_copy(i):
-        return pltpu.make_async_remote_copy(
-            src_ref=final.at[i, my_half], dst_ref=final.at[i, my_half],
-            send_sem=sum_send.at[i, 3], recv_sem=sum_recv.at[i, 3], device_id=partner, device_id_type=MESH)
-
     def return_start(i):
         wait_bytes(i, sum_recv.at[i, 2])
-        return_copy(i).start()
+        pieces(lambda at, size: pltpu.make_async_remote_copy(
+            src_ref=final.at[i, pl.ds(core * HALF + at, size)], dst_ref=final.at[i, pl.ds(core * HALF + at, size)],
+            send_sem=sum_send.at[i, 3], recv_sem=sum_recv.at[i, 3], device_id=partner, device_id_type=MESH))
 
     def out_copy(i):
         return pltpu.make_async_copy(final.at[i], grads_out[i], in_sems.at[2 + i])
 
     def out_start(i):
-        return_copy(i).wait_recv()
+        wait_half(i, sum_recv.at[i, 3])
         out_copy(i).start()
 
     local(0).wait()
@@ -358,7 +366,7 @@
     mask_rows(xp, 1)
     conv_stage(xp, 1, wp.at[0], 64, 4, 4, first_step)
     mask_rows(one)
-    conv_stage(one, 0, wp.at[1], 1, PAIRS - 2, 11, forward_epilogue(a_two, two))
+    conv_stage(one, 0, wp.at[1], 1, PAIRS - 2, 22, forward_epilogue(a_two, two))
     mask_rows(two)
     local(1).wait()
     halo_do(1, over, 0, 'recv')
@@ -369,19 +377,23 @@
     mask_rows(gp)
     d_two[0, 1] = zero_row
     d_two[PAIRS - 1, 0] = zero_row
-    conv_stage(gp, 0, wp.at[3], 1, PAIRS - 2, 11, backward_epilogue(a_two, d_two))
+    conv_stage(gp, 0, wp.at[3], 1, PAIRS - 2, 22, backward_epilogue(a_two, d_two))
     mask_rows(d_two)
 
     def call(fn, i):
         return lambda: fn(i)
 
     wgrad_stage(two, 0, gp, own_mask, acc, part.at[2], 16)
-    conv_stage(d_two, 0, wp.at[4], 1, PAIRS - 2, 11, backward_epilogue(a_one, d_one),
-               [(0, call(pair_start, 2)), (2, call(pair_add, 2)), (3, call(chunk_start, 2))])
+    pair_start(2)
+    wgrad_stage(one, 0, d_two, own_mask, acc, part.at[1], 16,
+                [(1, call(pair_add, 2)), (1, call(chunk_start, 2))])
+    pair_start(1)
+    conv_stage(d_two, 0, wp.at[4], 1, PAIRS - 2, 22, backward_epilogue(a_one, d_one),
+               [(0, call(pair_add, 1)), (0, call(chunk_start, 1)), (1, call(chunk_add, 2)), (1, call(spread_start, 2))])
     mask_rows(d_one)
-    wgrad_stage(one, 0, d_two, own_mask, acc, part.at[1], 16, [(2, call(chunk_add, 2)), (3, call(spread_start, 2))])
     wgrad_stage(xp, 1, d_one, own_mask, acc, part.at[0], 16,
-                [(0, call(pair_start, 1)), (1, call(pair_add, 1)), (2, call(chunk_start, 1)), (3, call(return_start, 2))])
+                [(1, call(chunk_add, 1)), (1, call(spread_start, 1)), (3, call(return_start, 2))])
+    pair_start(0)
 
     per_out = 8
     out_steps = OWN_PAIRS // per_out
@@ -419,16 +431,16 @@
             store(dst, s, s % 2).wait()
 
     final_stage(two, wp.at[2], xp, 1, block_out,
-                [(0, call(pair_start, 0)), (1, call(pair_add, 0)), (2, call(chunk_start, 0)), (3, call(chunk_add, 1)),
-                 (4, call(spread_start, 1)), (5, call(out_start, 2)), (7, call(chunk_add, 0))])
+                [(1, call(pair_add, 0)), (1, call(chunk_start, 0)), (4, call(out_start, 2)), (6, call(return_start, 1)),
+                 (7, call(chunk_add, 0)), (7, call(spread_start, 0))])
     final_stage(d_one, wp.at[5], gp, 0, grad_image,
-                [(0, call(spread_start, 0)), (3, call(return_start, 1)), (5, call(out_start, 1)), (6, call(return_start, 0))])
+                [(1, call(out_start, 1)), (5, call(return_start, 0))])
     out_start(0)
     for i in range(3):
-        pair_copy(i).wait_send()
+        wait_half(i, sum_send.at[i, 0])
         wait_bytes(i, sum_send.at[i, 1])
         wait_bytes(i, sum_send.at[i, 2])
-        return_copy(i).wait_send()
+        wait_half(i, sum_send.at[i, 3])
     for i in range(2):
         halo_do(i, over, 0, 'send')
         for chunk in range(SIDES):
@@ -436,6 +448,27 @@
         halo_do(i, under, 0, 'send')
     for i in range(3):
         out_copy(i).wait()
+
+
+def copy_kernel(*refs):
+    count = len(COPY_PARTS)
+    srcs, dsts, bufs = refs[:count], refs[count:2 * count], refs[2 * count:3 * count]
+    in_sems, out_sems = refs[3 * count:]
+    moves = []
+    for a, parts in enumerate(COPY_PARTS):
+        rows = srcs[a].shape[0] // parts
+        for b in range(parts):
+            piece = pl.ds(b * rows, rows)
+            n = len(moves)
+            moves.append((pltpu.make_async_copy(srcs[a].at[piece], bufs[a].at[piece], in_sems.at[n]),
+                          pltpu.make_async_copy(bufs[a].at[piece], dsts[a].at[piece], out_sems.at[n])))
+    for into, _ in moves:
+        into.start()
+    for into, back in moves:
+        into.wait()
+        back.start()
+    for _, back in moves:
+        back.wait()
 
 
 def solution(mesh):
@@ -481,11 +514,22 @@
         name='block',
     )
 
+    copy = pl.pallas_call(
+        copy_kernel,
+        out_shape=(tile_shape, tile_shape, dw_shape, dw_shape, dw_shape),
+        in_specs=[hbm] * 5,
+        out_specs=(hbm,) * 5,
+        scratch_shapes=[pltpu.VMEM(tile_shape.shape, BF16)] * 2 + [pltpu.VMEM(dw_shape.shape, F32)] * 3
+        + [pltpu.SemaphoreType.DMA((sum(COPY_PARTS),))] * 2,
+        compiler_params=pltpu.CompilerParams(vmem_limit_bytes=67043328),
+        name='hand_over',
+    )
+
     def local_block(image, w_first, w_second, w_third, grad_out):
         views = []
         for tile in (image, grad_out):
             views += [tile.reshape(TILE, TILE, CH), tile.reshape(TILE, TILE // QUAD, QUAD, CH), tile.reshape(OWN_PAIRS, 2, TILE // STRIPS, STRIPS, CH)]
-        out, dx, dw1, dw2, dw3 = call(*views, w_first, w_second, w_third)
+        out, dx, dw1, dw2, dw3 = copy(*call(*views, w_first, w_second, w_third))
         shape = (3, 3, CH, CH)
         return out[None], dx[None], dw1.reshape(shape), dw2.reshape(shape), dw3.reshape(shape)
 

time: 110 us -> 102 us (0.927)
  local copies, waits for them, and re-layouts: 9.42 us -> 0 us
    unnamed x13 -> x0, local copies, waits for them, and re-layouts: 9.42 us -> none
    pallas_call x1 -> x2, Pallas kernels: 100 us -> 101 us  [local_block(): out, dx, dw1, dw2, dw3 = copy(*call(*views, w_first, w_second, w_third))]
where the time goes in v4:
time: 102 us
  Pallas kernels  101 us (99%)
    pallas_call x2, Pallas kernels, local_block(): out, dx, dw1, dw2, dw3 = copy(*call(*views, w_first, w_second, w_third))  101 us

profile of v4, /device:TPU:0, one launch (start us, length us, event | category | flops | bytes accessed | tf_op | source)
XLA Modules:
  0.0 102.2 jit_solution(17944022561535652972)
XLA Ops:
  0.6 93.5 %block.1 = (bf16[128,128,128]{2,1,0:T(8,128)(2,1)}, bf16[128,128,128]{2,1,0:T(8,128)(2,1)}, f32[1152,128]{1,0:T(8,128)}, f32[1152,128]{1,0:T(8,128)}, f32[1152,128]{1,0:T(8,128)}) custom-call(bf16[128,128,128]{2,1,0:T(8,128)(2,1)} %bitcast.11, bf16[128,32,4,128]{3,2,1,0:T(4,128)(2,1)} %bitcast.12, bf16[64,2,8,16,128]{4,3,2,1,0:T(8,128)(2,1)} %bitcast.13, ...), custom_call_target="tpu_custom_call" | custom-call | tf_op jit(solution)/shard_map/block/pallas_call | solution.py:532
  94.1 7.9 %hand_over.1 = (bf16[128,128,128]{2,1,0:T(8,128)(2,1)}, bf16[128,128,128]{2,1,0:T(8,128)(2,1)}, f32[1152,128]{1,0:T(8,128)}, f32[1152,128]{1,0:T(8,128)}, f32[1152,128]{1,0:T(8,128)}) custom-call(bf16[128,128,128]{2,1,0:T(8,128)(2,1)} %get-tuple-element.15.refs_0_, bf16[128,128,128]{2,1,0:T(8,128)(2,1)} %get-tuple-element.16.refs_1_, ...), custom_call_target="tpu_custom_call" | custom-call | tf_op jit(solution)/shard_map/hand_over/pallas_call | solution.py:532

commit v5 on v3

--- a/solution.py
+++ b/solution.py
@@ -27,19 +27,26 @@
 QUAD = 4
 N_ROWS = 4
 N_COLS = 4
+UNITS = ((0, 0, 6 * CH), (1, 0, 9 * CH), (2, 0, 9 * CH), (0, 6 * CH, 3 * CH))
+OUT_ROWS = 16
 SIDES = 4
 SIDE_ROWS = TILE // SIDES
 HALF = 9 * CH // 2
 CHUNK = 9 * CH // (N_ROWS * N_COLS)
 
 
+def gelu_arg(value, square):
+    return jnp.tanh(value * (GELU_SCALE + (GELU_SCALE * GELU_CUBIC) * square))
+
+
 def gelu_tanh(value):
-    return 0.5 * value * (1.0 + jnp.tanh(GELU_SCALE * (value + GELU_CUBIC * value * value * value)))
+    return 0.5 * value * (1.0 + gelu_arg(value, value * value))
 
 
 def gelu_slope(value):
-    tanh_val = jnp.tanh(GELU_SCALE * (value + GELU_CUBIC * value * value * value))
-    return 0.5 * (1.0 + tanh_val) + 0.5 * value * (1.0 - tanh_val * tanh_val) * GELU_SCALE * (1.0 + 3.0 * GELU_CUBIC * value * value)
+    square = value * value
+    s = 0.5 + 0.5 * gelu_arg(value, square)
+    return s + (s * (1.0 - s) * value) * (2.0 * GELU_SCALE + (6.0 * GELU_SCALE * GELU_CUBIC) * square)
 
 
 def row_at(ref, k, r, off):
@@ -92,7 +99,7 @@
     return jnp.concatenate([left, value, right], axis=0)
 
 
-def wgrad_stage(val, off, grad, own_mask, acc, out, per_step, hooks=()):
+def wgrad_stage(val, off, grad, own_mask, acc, out, per_step, hooks=(), do_pair=True, do_last=True):
     dims = (((0,), (0,)), ((), ()))
     flat = per_step * STEPS * STRIPS
     acc[...] = jnp.zeros_like(acc)
@@ -108,19 +115,20 @@
         for par in range(2):
             d = grad[pl.ds(k, per_step), par] * own_mask[...][None]
             shifted.append([d[:, 2 - q:2 - q + STEPS].reshape(flat, CH) for q in range(3)])
-        lhs = jnp.concatenate([jnp.concatenate(rows[par:par + 3], axis=1) for par in range(2)], axis=0)
-        rhs = jnp.concatenate([jnp.concatenate(shifted[par][:2], axis=1) for par in range(2)], axis=0)
-        acc[:, 0:2 * CH] += lax.dot_general(lhs, rhs, dims, preferred_element_type=F32)
-        both = jnp.concatenate([shifted[0][2], shifted[1][2]], axis=1)
-        last = lax.dot_general(jnp.concatenate(rows, axis=1), both, dims, preferred_element_type=F32)
-        acc[:, 2 * CH:3 * CH] += last[0:3 * CH, 0:CH] + last[CH:4 * CH, CH:2 * CH]
+        if do_pair:
+            lhs = jnp.concatenate([jnp.concatenate(rows[par:par + 3], axis=1) for par in range(2)], axis=0)
+            rhs = jnp.concatenate([jnp.concatenate(shifted[par][:2], axis=1) for par in range(2)], axis=0)
+            acc[:, 0:2 * CH] += lax.dot_general(lhs, rhs, dims, preferred_element_type=F32)
+        if do_last:
+            both = jnp.concatenate([shifted[0][2], shifted[1][2]], axis=1)
+            last = lax.dot_general(jnp.concatenate(rows, axis=1), both, dims, preferred_element_type=F32)
+            acc[:, 2 * CH:3 * CH] += last[0:3 * CH, 0:CH] + last[CH:4 * CH, CH:2 * CH]
         run_hooks(hooks, step)
         return carry
 
     lax.fori_loop(0, OWN_PAIRS // per_step, body, 0)
-    for p in range(3):
-        for q in range(3):
-            out[(p * 3 + q) * CH:(p * 3 + q + 1) * CH] = acc[p * CH:(p + 1) * CH, q * CH:(q + 1) * CH]
+    for q in ([0, 1] if do_pair else []) + ([2] if do_last else []):
+        out[q * 3 * CH:(q + 1) * 3 * CH] = acc[:, q * CH:(q + 1) * CH]
 
 
 def directions():
@@ -128,10 +136,10 @@
 
 
 def block_kernel(image, image_quads, image_pairs, grad, grad_quads, grad_pairs, w_first, w_second, w_third,
-                 block_out, grad_image, dw_first, dw_second, dw_third,
-                 xp, one, two, gp, d_two, d_one, a_one, a_two, wp,
-                 halo, wide, outs, acc, img_mask, own_mask, part, pair_got, half, got, final,
-                 in_sems, out_sems, halo_send, halo_recv, sum_send, sum_recv):
+                 a_one, a_two, final,
+                 xp, one, two, gp, d_two, d_one, wp,
+                 halo, wide, acc, img_mask, own_mask, part, pair_got, half, got,
+                 in_sems, halo_send, halo_recv, sum_send, sum_recv):
     n_rows, n_cols = N_ROWS, N_COLS
     n_dev = n_rows * n_cols
     row_id = lax.axis_index('row')
@@ -225,8 +233,9 @@
                     copy.wait_send()
 
     def halo_start(i):
+        halo_do(i, sides, 0, 'start')
         halo_do(i, over, 0, 'start')
-        for chunk in range(SIDES):
+        for chunk in range(1, SIDES):
             halo_do(i, sides, chunk, 'start')
         halo_do(i, under, 0, 'start')
 
@@ -277,22 +286,30 @@
     chip = col_id * 2 + row_id // 2
     n_chips = n_dev // 2
     partner = {'col': col_id, 'row': row_id + 1 - 2 * core}
-    my_half = pl.ds(core * HALF, HALF)
-    mine = pl.ds(core * HALF + chip * CHUNK, CHUNK)
     MESH = pl.DeviceIdType.MESH
-    grads_out = (dw_first, dw_second, dw_third)
-
-    def pair_copy(i):
-        return pltpu.make_async_remote_copy(
-            src_ref=part.at[i, pl.ds((1 - core) * HALF, HALF)], dst_ref=pair_got.at[i],
-            send_sem=sum_send.at[i, 0], recv_sem=sum_recv.at[i, 0], device_id=partner, device_id_type=MESH)
-
-    def pair_start(i):
-        pair_copy(i).start()
-
-    def pair_add(i):
-        pair_copy(i).wait_recv()
-        half[i] = part[i, my_half] + pair_got[i]
+
+    def pair_start(u):
+        i, base, rows = UNITS[u]
+        pltpu.make_async_remote_copy(
+            src_ref=part.at[i, pl.ds(base + (1 - core) * (rows // 2), rows // 2)],
+            dst_ref=pair_got.at[i, pl.ds(base // 2, rows // 2)],
+            send_sem=sum_send.at[u, 0], recv_sem=sum_recv.at[u, 0], device_id=partner, device_id_type=MESH).start()
+
+    def wait_half(u, sem):
+        i, base, rows = UNITS[u]
+        ref = half.at[i, pl.ds(base // 2, rows // 2)]
+        pltpu.make_async_copy(ref, ref, sem).wait()
+
+    def wait_chunks(u, sem):
+        i, base, rows = UNITS[u]
+        ref = got.at[i, :, pl.ds(base // 16, rows // 16)]
+        pltpu.make_async_copy(ref, ref, sem).wait()
+
+    def pair_add(u):
+        i, base, rows = UNITS[u]
+        wait_half(u, sum_recv.at[u, 0])
+        there = pl.ds(base // 2, rows // 2)
+        half[i, there] = part[i, pl.ds(base + core * (rows // 2), rows // 2)] + pair_got[i, there]
 
     def to_chips(make):
         def body(d, carry):
@@ -301,41 +318,42 @@
             return carry
         lax.fori_loop(1, n_chips, body, 0)
 
-    def chunk_start(i):
+    def chunk_start(u):
+        i, base, rows = UNITS[u]
+        size = rows // 16
         to_chips(lambda d, other, ids: pltpu.make_async_remote_copy(
-            src_ref=half.at[i, pl.ds(other * CHUNK, CHUNK)], dst_ref=got.at[i, d - 1],
-            send_sem=sum_send.at[i, 1], recv_sem=sum_recv.at[i, 1], device_id=ids, device_id_type=MESH))
-
-    def wait_bytes(i, sem):
-        pltpu.make_async_copy(got.at[i], got.at[i], sem).wait()
-
-    def chunk_add(i):
-        wait_bytes(i, sum_recv.at[i, 1])
-        total = half[i, pl.ds(chip * CHUNK, CHUNK)]
+            src_ref=half.at[i, pl.ds(base // 2 + other * size, size)], dst_ref=got.at[i, d - 1, pl.ds(base // 16, size)],
+            send_sem=sum_send.at[u, 1], recv_sem=sum_recv.at[u, 1], device_id=ids, device_id_type=MESH))
+
+    def mine(u):
+        i, base, rows = UNITS[u]
+        return pl.ds(base + core * (rows // 2) + chip * (rows // 16), rows // 16)
+
+    def chunk_add(u):
+        i, base, rows = UNITS[u]
+        size = rows // 16
+        wait_chunks(u, sum_recv.at[u, 1])
+        total = half[i, pl.ds(base // 2 + chip * size, size)]
         for d in range(n_chips - 1):
-            total = total + got[i, d]
-        final[i, mine] = total
-
-    def spread_start(i):
+            total = total + got[i, d, base // 16:base // 16 + size]
+        final[i, mine(u)] = total
+
+    def spread_start(u):
+        i = UNITS[u][0]
         to_chips(lambda d, other, ids: pltpu.make_async_remote_copy(
-            src_ref=final.at[i, mine], dst_ref=final.at[i, mine],
-            send_sem=sum_send.at[i, 2], recv_sem=sum_recv.at[i, 2], device_id=ids, device_id_type=MESH))
-
-    def return_copy(i):
-        return pltpu.make_async_remote_copy(
-            src_ref=final.at[i, my_half], dst_ref=final.at[i, my_half],
-            send_sem=sum_send.at[i, 3], recv_sem=sum_recv.at[i, 3], device_id=partner, device_id_type=MESH)
-
-    def return_start(i):
-        wait_bytes(i, sum_recv.at[i, 2])
-        return_copy(i).start()
-
-    def out_copy(i):
-        return pltpu.make_async_copy(final.at[i], grads_out[i], in_sems.at[2 + i])
-
-    def out_start(i):
-        return_copy(i).wait_recv()
-        out_copy(i).start()
+            src_ref=final.at[i, mine(u)], dst_ref=final.at[i, mine(u)],
+            send_sem=sum_send.at[u, 2], recv_sem=sum_recv.at[u, 2], device_id=ids, device_id_type=MESH))
+
+    def return_start(u):
+        i, base, rows = UNITS[u]
+        wait_chunks(u, sum_recv.at[u, 2])
+        ref = final.at[i, pl.ds(base + core * (rows // 2), rows // 2)]
+        pltpu.make_async_remote_copy(
+            src_ref=ref, dst_ref=ref, send_sem=sum_send.at[u, 3], recv_sem=sum_recv.at[u, 3],
+            device_id=partner, device_id_type=MESH).start()
+
+    def return_wait(u):
+        wait_half(u, sum_recv.at[u, 3])
 
     local(0).wait()
     halo_do(0, over, 0, 'recv')
@@ -358,7 +376,7 @@
     mask_rows(xp, 1)
     conv_stage(xp, 1, wp.at[0], 64, 4, 4, first_step)
     mask_rows(one)
-    conv_stage(one, 0, wp.at[1], 1, PAIRS - 2, 11, forward_epilogue(a_two, two))
+    conv_stage(one, 0, wp.at[1], 1, PAIRS - 2, 22, forward_epilogue(a_two, two))
     mask_rows(two)
     local(1).wait()
     halo_do(1, over, 0, 'recv')
@@ -369,73 +387,78 @@
     mask_rows(gp)
     d_two[0, 1] = zero_row
     d_two[PAIRS - 1, 0] = zero_row
-    conv_stage(gp, 0, wp.at[3], 1, PAIRS - 2, 11, backward_epilogue(a_two, d_two))
+    conv_stage(gp, 0, wp.at[3], 1, PAIRS - 2, 22, backward_epilogue(a_two, d_two))
     mask_rows(d_two)
 
     def call(fn, i):
         return lambda: fn(i)
 
     wgrad_stage(two, 0, gp, own_mask, acc, part.at[2], 16)
-    conv_stage(d_two, 0, wp.at[4], 1, PAIRS - 2, 11, backward_epilogue(a_one, d_one),
-               [(0, call(pair_start, 2)), (2, call(pair_add, 2)), (3, call(chunk_start, 2))])
+    pair_start(2)
+    wgrad_stage(one, 0, d_two, own_mask, acc, part.at[1], 16,
+                [(1, call(pair_add, 2)), (1, call(chunk_start, 2))])
+    pair_start(1)
+    conv_stage(d_two, 0, wp.at[4], 1, PAIRS - 2, 22, backward_epilogue(a_one, d_one),
+               [(0, call(pair_add, 1)), (0, call(chunk_start, 1)), (1, call(chunk_add, 2)), (1, call(spread_start, 2))])
     mask_rows(d_one)
-    wgrad_stage(one, 0, d_two, own_mask, acc, part.at[1], 16, [(2, call(chunk_add, 2)), (3, call(spread_start, 2))])
     wgrad_stage(xp, 1, d_one, own_mask, acc, part.at[0], 16,
-                [(0, call(pair_start, 1)), (1, call(pair_add, 1)), (2, call(chunk_start, 1)), (3, call(return_start, 2))])
-
-    per_out = 8
-    out_steps = OWN_PAIRS // per_out
-
-    def store(dst, s, slot):
-        return pltpu.make_async_copy(outs.at[slot], dst.at[pl.ds(s * 2 * per_out, 2 * per_out)], out_sems.at[slot])
-
-    def final_stage(src, wp_ref, skip, skip_off, dst, hooks):
-        def body(s, carry):
-            slot = lax.rem(s, 2)
-
-            @pl.when(s >= 2)
-            def _():
-                store(dst, s - 2, slot).wait()
-            base = FIRST_OWN + s * per_out
-            for j in range(per_out):
-                k = base + j
-                parts = []
-                for q in range(3):
-                    for r in range(4):
-                        pair, par = row_at(src, k, r, 0)
-                        parts.append(src[pair, par, q:q + STEPS].reshape(STEPS * STRIPS, CH))
-                res = jnp.dot(jnp.concatenate(parts, axis=1), wp_ref[...], preferred_element_type=F32)
-                for par in range(2):
-                    value = res[:, par * CH:(par + 1) * CH].reshape(STEPS, STRIPS, CH) + skip[k + skip_off, par, 1:1 + STEPS].astype(F32)
-                    line = 2 * j + par
-                    for t in range(STEPS):
-                        wide[line, pl.ds(8 + t, STRIPS, stride=STEPS)] = value[t]
-                    outs[slot, line] = wide[line, 8 + COL_HALO:8 + COL_HALO + TILE].astype(BF16)
-            store(dst, s, slot).start()
-            run_hooks(hooks, s)
-            return carry
-        lax.fori_loop(0, out_steps, body, 0)
-        for s in range(out_steps - 2, out_steps):
-            store(dst, s, s % 2).wait()
-
-    final_stage(two, wp.at[2], xp, 1, block_out,
-                [(0, call(pair_start, 0)), (1, call(pair_add, 0)), (2, call(chunk_start, 0)), (3, call(chunk_add, 1)),
-                 (4, call(spread_start, 1)), (5, call(out_start, 2)), (7, call(chunk_add, 0))])
-    final_stage(d_one, wp.at[5], gp, 0, grad_image,
-                [(0, call(spread_start, 0)), (3, call(return_start, 1)), (5, call(out_start, 1)), (6, call(return_start, 0))])
-    out_start(0)
-    for i in range(3):
-        pair_copy(i).wait_send()
-        wait_bytes(i, sum_send.at[i, 1])
-        wait_bytes(i, sum_send.at[i, 2])
-        return_copy(i).wait_send()
+                [(2, call(chunk_add, 1)), (2, call(spread_start, 1))], do_last=False)
+    pair_start(0)
+    wgrad_stage(xp, 1, d_one, own_mask, acc, part.at[0], 32,
+                [(0, call(return_start, 2)), (1, call(pair_add, 0)), (1, call(chunk_start, 0))], do_pair=False)
+    pair_start(3)
+
+    def final_epilogue(skip, off, post):
+        def epilogue(k, par, j, value):
+            post[k, par] = (value + skip[k + off, par, 1:1 + STEPS].astype(F32)).astype(BF16)
+        return epilogue
+
+    conv_stage(two, 0, wp.at[2], FIRST_OWN, OWN_PAIRS, 16, final_epilogue(xp, 1, a_one),
+               [(0, call(pair_add, 3)), (0, call(chunk_start, 3)), (2, call(return_start, 1)), (2, call(chunk_add, 0)),
+                (2, call(spread_start, 0)), (3, call(chunk_add, 3)), (3, call(spread_start, 3))])
+    conv_stage(d_one, 0, wp.at[5], FIRST_OWN, OWN_PAIRS, 16, final_epilogue(gp, 0, a_two),
+               [(2, call(return_start, 0)), (2, call(return_start, 3))])
+    for u in range(len(UNITS)):
+        return_wait(u)
+        wait_half(u, sum_send.at[u, 0])
+        wait_chunks(u, sum_send.at[u, 1])
+        wait_chunks(u, sum_send.at[u, 2])
+        wait_half(u, sum_send.at[u, 3])
     for i in range(2):
         halo_do(i, over, 0, 'send')
         for chunk in range(SIDES):
             halo_do(i, sides, chunk, 'send')
         halo_do(i, under, 0, 'send')
-    for i in range(3):
-        out_copy(i).wait()
+
+
+def hand_over_kernel(y_strips, dx_strips, sums, block_out, grad_image, dw_first, dw_second, dw_third,
+                     wide, lines, sems, dw_sems):
+    dw_copies = [
+        pltpu.make_async_copy(sums.at[i, pl.ds((q * 3 + p) * CH, CH)], dw.at[pl.ds((p * 3 + q) * CH, CH)], dw_sems.at[i, p * 3 + q])
+        for i, dw in enumerate((dw_first, dw_second, dw_third)) for p in range(3) for q in range(3)]
+    for copy in dw_copies:
+        copy.start()
+
+    for a, (strips, dst) in enumerate(((y_strips, block_out), (dx_strips, grad_image))):
+        def store(b):
+            return pltpu.make_async_copy(lines.at[a, b], dst.at[pl.ds(b * OUT_ROWS, OUT_ROWS)], sems.at[a, b])
+
+        def body(b, carry):
+            for r in range(OUT_ROWS):
+                k, par = FIRST_OWN + b * (OUT_ROWS // 2) + r // 2, r % 2
+                for t in range(STEPS):
+                    wide[r, pl.ds(8 + t, STRIPS, stride=STEPS)] = strips[k, par, t].astype(F32)
+            for r in range(OUT_ROWS):
+                lines[a, b, r] = wide[r, 8 + COL_HALO:8 + COL_HALO + TILE].astype(BF16)
+            store(b).start()
+            return carry
+        lax.fori_loop(0, TILE // OUT_ROWS, body, 0)
+
+    for a, dst in enumerate((block_out, grad_image)):
+        for b in range(TILE // OUT_ROWS):
+            pltpu.make_async_copy(lines.at[a, b], dst.at[pl.ds(b * OUT_ROWS, OUT_ROWS)], sems.at[a, b]).wait()
+    for copy in dw_copies:
+        copy.wait()
 
 
 def solution(mesh):
@@ -450,18 +473,16 @@
     n_dev = N_ROWS * N_COLS
     call = pl.pallas_call(
         block_kernel,
-        out_shape=(tile_shape, tile_shape, dw_shape, dw_shape, dw_shape),
+        out_shape=(pltpu.VMEM(plain, BF16), pltpu.VMEM(plain, BF16), pltpu.VMEM((3, 9 * CH, CH), F32)),
         in_specs=[hbm] * 6 + [vmem] * 3,
-        out_specs=(hbm,) * 5,
+        out_specs=(vmem,) * 3,
         scratch_shapes=[
             pltpu.VMEM((PAIRS + 2, 2, PAD_STEPS, STRIPS, CH), BF16),
             pltpu.VMEM(padded, BF16), pltpu.VMEM(padded, BF16), pltpu.VMEM(padded, BF16),
             pltpu.VMEM(padded, BF16), pltpu.VMEM(padded, BF16),
-            pltpu.VMEM(plain, BF16), pltpu.VMEM(plain, BF16),
             pltpu.VMEM((6, 12 * CH, 2 * CH), BF16),
             pltpu.VMEM((2, 2, EXT_ROWS, QUAD, CH), BF16),
             pltpu.VMEM((16, EXT_COLS + 16, CH), F32),
-            pltpu.VMEM((2, 16, TILE, CH), BF16),
             pltpu.VMEM((3 * CH, 3 * CH), F32),
             pltpu.VMEM((PAD_STEPS, STRIPS, CH), BF16),
             pltpu.VMEM((PAD_STEPS, STRIPS, CH), BF16),
@@ -469,23 +490,36 @@
             pltpu.VMEM((3, HALF, CH), F32),
             pltpu.VMEM((3, HALF, CH), F32),
             pltpu.VMEM((3, n_dev // 2 - 1, CHUNK, CH), F32),
-            pltpu.VMEM((3, 9 * CH, CH), F32),
-            pltpu.SemaphoreType.DMA((5,)),
             pltpu.SemaphoreType.DMA((2,)),
             pltpu.SemaphoreType.DMA((2, 8, SIDES)),
             pltpu.SemaphoreType.DMA((2, 8, SIDES)),
-            pltpu.SemaphoreType.DMA((3, 4)),
-            pltpu.SemaphoreType.DMA((3, 4)),
+            pltpu.SemaphoreType.DMA((len(UNITS), 4)),
+            pltpu.SemaphoreType.DMA((len(UNITS), 4)),
         ],
-        compiler_params=pltpu.CompilerParams(vmem_limit_bytes=67043328, collective_id=0, has_side_effects=True),
+        compiler_params=pltpu.CompilerParams(vmem_limit_bytes=54500000, collective_id=0, has_side_effects=True),
         name='block',
+    )
+
+    hand_over = pl.pallas_call(
+        hand_over_kernel,
+        out_shape=(tile_shape, tile_shape, dw_shape, dw_shape, dw_shape),
+        in_specs=[vmem] * 3,
+        out_specs=(hbm,) * 5,
+        scratch_shapes=[
+            pltpu.VMEM((OUT_ROWS, EXT_COLS + 16, CH), F32),
+            pltpu.VMEM((2, TILE // OUT_ROWS, OUT_ROWS, TILE, CH), BF16),
+            pltpu.SemaphoreType.DMA((2, TILE // OUT_ROWS)),
+            pltpu.SemaphoreType.DMA((3, 9)),
+        ],
+        compiler_params=pltpu.CompilerParams(vmem_limit_bytes=32 * 2**20),
+        name='hand_over',
     )
 
     def local_block(image, w_first, w_second, w_third, grad_out):
         views = []
         for tile in (image, grad_out):
             views += [tile.reshape(TILE, TILE, CH), tile.reshape(TILE, TILE // QUAD, QUAD, CH), tile.reshape(OWN_PAIRS, 2, TILE // STRIPS, STRIPS, CH)]
-        out, dx, dw1, dw2, dw3 = call(*views, w_first, w_second, w_third)
+        out, dx, dw1, dw2, dw3 = hand_over(*call(*views, w_first, w_second, w_third))
         shape = (3, 3, CH, CH)
         return out[None], dx[None], dw1.reshape(shape), dw2.reshape(shape), dw3.reshape(shape)
 

time: 110 us -> 95.3 us (0.87)
  local copies, waits for them, and re-layouts: 9.42 us -> 0 us
  Pallas kernels: 100 us -> 94.4 us
    unnamed x13 -> x0, local copies, waits for them, and re-layouts: 9.42 us -> none
    pallas_call x1 -> x2, Pallas kernels: 100 us -> 94.4 us  [the longest x1 90.2 us: local_block(): call(*views, w_first, w_second, w_third)]
where the time goes in v5:
time: 95.3 us; the launch traced here: 95.2 us
  Pallas kernels  94.4 us (99%)
    pallas_call x1, Pallas kernels, local_block(): call(*views, w_first, w_second, w_third)  90.2 us
    pallas_call x1, Pallas kernels, local_block(): hand_over(*call(*views, w_first, w_second, w_third))  4.23 us

profile of v5, /device:TPU:0, one launch (start us, length us, event | category | flops | bytes accessed | tf_op | source)
XLA Modules:
  0.0 95.2 jit_solution(11302987308605707681)
XLA Ops:
  0.6 90.2 %block.1 = (bf16[68,2,9,16,128]{4,3,2,1,0:T(8,128)(2,1)S(1)}, bf16[68,2,9,16,128]{4,3,2,1,0:T(8,128)(2,1)S(1)}, f32[3,1152,128]{2,1,0:T(8,128)S(1)}) custom-call(bf16[128,128,128]{2,1,0:T(8,128)(2,1)} %bitcast.11, bf16[128,32,4,128]{3,2,1,0:T(4,128)(2,1)} %bitcast.12, bf16[64,2,8,16,128]{4,3,2,1,0:T(8,128)(2,1)} %bitcast.13, ...), custom_call_target="tpu_custom_call" | custom-call | tf_op jit(solution)/shard_map/block/pallas_call | solution.py:522
  90.8 4.2 %hand_over.1 = (bf16[128,128,128]{2,1,0:T(8,128)(2,1)}, bf16[128,128,128]{2,1,0:T(8,128)(2,1)}, f32[1152,128]{1,0:T(8,128)}, f32[1152,128]{1,0:T(8,128)}, f32[1152,128]{1,0:T(8,128)}) custom-call(bf16[68,2,9,16,128]{4,3,2,1,0:T(8,128)(2,1)S(1)} %get-tuple-element.13.y_strips, bf16[68,2,9,16,128]{4,3,2,1,0:T(8,128)(2,1)S(1)} %get-tuple-element.14.dx_strips, ...), custom_call_target="tpu_custom_call" | custom-call | tf_op jit(solution)/shard_map/hand_over/pallas_call | solution.py:522

commit v6 on v5

--- a/solution.py
+++ b/solution.py
@@ -393,10 +393,10 @@
     def call(fn, i):
         return lambda: fn(i)
 
-    wgrad_stage(two, 0, gp, own_mask, acc, part.at[2], 16)
+    wgrad_stage(two, 0, gp, own_mask, acc, part.at[2], 32)
     pair_start(2)
-    wgrad_stage(one, 0, d_two, own_mask, acc, part.at[1], 16,
-                [(1, call(pair_add, 2)), (1, call(chunk_start, 2))])
+    wgrad_stage(one, 0, d_two, own_mask, acc, part.at[1], 32,
+                [(0, call(pair_add, 2)), (0, call(chunk_start, 2))])
     pair_start(1)
     conv_stage(d_two, 0, wp.at[4], 1, PAIRS - 2, 22, backward_epilogue(a_one, d_one),
                [(0, call(pair_add, 1)), (0, call(chunk_start, 1)), (1, call(chunk_add, 2)), (1, call(spread_start, 2))])

time: 95.3 us -> 94.4 us (level)
  no operation moved by 1% of the time
where the time goes in v6:
time: 94.4 us; the launch traced here: 94.3 us
  Pallas kernels  93.5 us (99%)
    pallas_call x1, Pallas kernels, local_block(): call(*views, w_first, w_second, w_third)  89.3 us
    pallas_call x1, Pallas kernels, local_block(): hand_over(*call(*views, w_first, w_second, w_third))  4.23 us

profile of v6, /device:TPU:0, one launch (start us, length us, event | category | flops | bytes accessed | tf_op | source)
XLA Modules:
  0.0 94.3 jit_solution(12412083348753937784)
XLA Ops:
  0.6 89.3 %block.1 = (bf16[68,2,9,16,128]{4,3,2,1,0:T(8,128)(2,1)S(1)}, bf16[68,2,9,16,128]{4,3,2,1,0:T(8,128)(2,1)S(1)}, f32[3,1152,128]{2,1,0:T(8,128)S(1)}) custom-call(bf16[128,128,128]{2,1,0:T(8,128)(2,1)} %bitcast.11, bf16[128,32,4,128]{3,2,1,0:T(4,128)(2,1)} %bitcast.12, bf16[64,2,8,16,128]{4,3,2,1,0:T(8,128)(2,1)} %bitcast.13, ...), custom_call_target="tpu_custom_call" | custom-call | tf_op jit(solution)/shard_map/block/pallas_call | solution.py:522
  89.9 4.2 %hand_over.1 = (bf16[128,128,128]{2,1,0:T(8,128)(2,1)}, bf16[128,128,128]{2,1,0:T(8,128)(2,1)}, f32[1152,128]{1,0:T(8,128)}, f32[1152,128]{1,0:T(8,128)}, f32[1152,128]{1,0:T(8,128)}) custom-call(bf16[68,2,9,16,128]{4,3,2,1,0:T(8,128)(2,1)S(1)} %get-tuple-element.13.y_strips, bf16[68,2,9,16,128]{4,3,2,1,0:T(8,128)(2,1)S(1)} %get-tuple-element.14.dx_strips, ...), custom_call_target="tpu_custom_call" | custom-call | tf_op jit(solution)/shard_map/hand_over/pallas_call | solution.py:522
